TPU v7x, 32 devices: a whole 2x2x4 slice. The times are simulated.
32 devices in a mesh: slab: 4 (over z), sub: 8 (over y, x, core).
Axes of the slice: x: 2, y: 2, z: 4, core: 2. Of those that a mesh axis runs over, the one named last changes fastest.
Arguments:
- near_null: float32 [18, 16384], P(None, ('slab', 'sub')), may hold values from -48 to 48
- aggregates: int32 [16384], P(('slab', 'sub')), may hold values from 0 to 63
- diag_block: float32 [9, 16384], P(None, ('slab', 'sub')), may hold values from -1 to 12, as said below
- off_blocks: float32 [26, 9, 16384], P(None, None, ('slab', 'sub')), may hold values from -18 to 18
- columns: int32 [26, 16384], P(None, ('slab', 'sub')), may hold values from 0 to 767, as said below
- sends: int32 [4, 2048], P(None, ('slab', 'sub')), may hold values from 0 to 511
- start_vector: float32 [3, 16384], P(None, ('slab', 'sub')), may hold values from -18 to 18
Outputs:
- prolong_off: bfloat16 [26, 18, 16384], P(None, None, ('slab', 'sub'))
- prolong_self: bfloat16 [18, 16384], P(None, ('slab', 'sub'))
- rho: float32 [], replicated
Inputs may be any that keep to these rules, and one draw needn't show every extreme that they name: `diag_block`: each block, read as 3x3 row-major, is symmetric with diagonal entries between 6 and 12 and off-diagonal entries between -1 and 1. `columns`: entries below 512 name a node of the same device; an entry c of 512 or more names ghost slot c - 512. Row e lists, for each device, the local rows it sends to its neighbour at sub + 1, sub - 1, slab + 1, slab - 1 for e = 0, 1, 2, 3. `aggregates`: aggregates lie within one device.
All inputs are finite; a program needn't handle non-finite values.
Results may differ from a plain program's by a relative error of at most 0.001.
Values sent between devices are 32-bit elements; how exact they have to be, the bound alone decides.
A program may use at most 64 MiB of HBM per device.

v0:
```python
import functools

import jax
import jax.numpy as jnp
from jax import lax
from jax.experimental import pallas as pl
from jax.experimental.pallas import tpu as pltpu
from jax.sharding import PartitionSpec as P

ITERS = 8
OMEGA = 4.0 / 3.0
LANES = 128
MESH = pl.DeviceIdType.MESH


def lane_gather(table, lanes):
    return jnp.take_along_axis(table, lanes, axis=1, mode="promise_in_bounds")


def tile(number):
    return pl.ds(number * LANES, LANES)


def pick(tables, index, first):
    high = index >> 7
    low = index & (LANES - 1)
    out = jnp.zeros(index.shape, jnp.float32)
    for step, table in enumerate(tables):
        out = jnp.where(high == first + step, lane_gather(table, low), out)
    return out


def invert_rows(entries):
    cofactor = [
        entries[4] * entries[8] - entries[5] * entries[7],
        entries[5] * entries[6] - entries[3] * entries[8],
        entries[3] * entries[7] - entries[4] * entries[6],
        entries[2] * entries[7] - entries[1] * entries[8],
        entries[0] * entries[8] - entries[2] * entries[6],
        entries[1] * entries[6] - entries[0] * entries[7],
        entries[1] * entries[5] - entries[2] * entries[4],
        entries[2] * entries[3] - entries[0] * entries[5],
        entries[0] * entries[4] - entries[1] * entries[3],
    ]
    determinant = entries[0] * cofactor[0] + entries[1] * cofactor[1] + entries[2] * cofactor[2]
    return [
        cofactor[column * 3 + row] / determinant for row in range(3) for column in range(3)
    ]


def unit_places(slots, tiles):
    units = []
    for k in range(0, slots - 7, 8):
        for j in range(tiles):
            units.append([(0, k, 8, j)])
    rest = slots % 8
    if rest:
        share = 8 // rest
        for j in range(0, tiles, share):
            units.append(
                [
                    (rest * i, slots - rest, rest, j + i)
                    for i in range(min(share, tiles - j))
                ]
            )
    return units


def scale_kernel(raw_ref, tent_ref, rho_ref, off_ref, self_ref):
    slots, rows = off_ref.shape[1:]
    inverse = OMEGA / rho_ref[...]
    factor = jnp.broadcast_to(-inverse, (8, LANES))
    places = unit_places(slots, rows // LANES)
    for j in range(rows // LANES):
        for entry in range(off_ref.shape[0]):
            parts = [
                (raw_ref[entry, u] * factor)[at : at + count]
                for u in range(len(places))
                for at, k, count, tile_number in places[u]
                if tile_number == j
            ]
            off_ref[entry, :, tile(j)] = jnp.concatenate(parts, axis=0).astype(off_ref.dtype)
    self_ref[...] = ((1.0 - inverse) * tent_ref[...]).astype(self_ref.dtype)


def kernel(
    n_slab, n_sub,
    near_hbm, agg_hbm, diag_hbm, off_hbm, cols_hbm, sends_hbm, start_hbm,
    raw_hbm, tent_ref, rho_ref,
    near_ref, agg_ref, diag_ref, cols_ref, sends_ref, start_ref, raw_ref, off_v, cols_u, mats, dinv, text, hist, sidx,
    sendw, recvw, sendt, recvt, stat, stats,
    off_sem, raw_sem, sendw_sem, recvw_sem, sendt_sem, recvt_sem,
    ss_sem, rs_sem,
):
    slots, rows = cols_ref.shape
    half = sends_ref.shape[1]
    tiles = rows // LANES
    units = unit_places(slots, tiles)
    modes = near_ref.shape[0] // 3
    groups = rows // 8
    a = lax.axis_index("slab")
    b = lax.axis_index("sub")
    loads = [
        pltpu.make_async_copy(source, target, off_sem.at[number])
        for number, (source, target) in enumerate(
            (
                (start_hbm, start_ref),
                (sends_hbm, sends_ref),
                (agg_hbm, agg_ref),
                (near_hbm, near_ref),
                (diag_hbm, diag_ref),
                (cols_hbm, cols_ref),
                (off_hbm, off_v),
            )
        )
    ]
    for load in loads:
        load.start()

    recvw[...] = jnp.zeros_like(recvw)
    recvt[...] = jnp.zeros_like(recvt)
    barrier = pltpu.get_barrier_semaphore()

    def greet(step, unused):
        target = lax.rem(a * n_sub + b + step, n_slab * n_sub)
        pl.semaphore_signal(
            barrier, inc=1,
            device_id={"slab": lax.div(target, n_sub), "sub": lax.rem(target, n_sub)},
            device_id_type=MESH,
        )
        return unused

    lax.fori_loop(1, n_slab * n_sub, greet, 0)

    ways = (
        ("sub", b + 1, 0, b < n_sub - 1, b > 0),
        ("sub", b - 1, 0, b > 0, b < n_sub - 1),
        ("slab", a + 1, 1, a < n_slab - 1, a > 0),
        ("slab", a - 1, 1, a > 0, a < n_slab - 1),
    )

    def w_copy(t, way):
        axis, target, pair, unused, unused2 = ways[way]
        return pltpu.make_async_remote_copy(
            src_ref=sendw.at[t, pair], dst_ref=recvw.at[t, way],
            send_sem=sendw_sem.at[t, way], recv_sem=recvw_sem.at[t, way],
            device_id={axis: target}, device_id_type=MESH,
        )

    def t_copy(way):
        axis, target, pair, unused, unused2 = ways[way]
        return pltpu.make_async_remote_copy(
            src_ref=sendt.at[pair], dst_ref=recvt.at[way],
            send_sem=sendt_sem.at[way], recv_sem=recvt_sem.at[way],
            device_id={axis: target}, device_id_type=MESH,
        )

    def each_target(make, act):
        for way in range(4):
            pl.when(ways[way][3])(functools.partial(act, make, way))

    def each_source(make):
        for way in range(4):
            pl.when(ways[way][4])(functools.partial(lambda way: make(way).wait_recv(), way))

    hist[...] = jnp.zeros_like(hist)
    loads[0].wait()
    loads[1].wait()
    hist[0, 0:3, :] = start_ref[...]
    for pair in range(2):
        sidx[pair] = jnp.broadcast_to(
            jnp.concatenate(
                [sends_ref[2 * pair : 2 * pair + 1, :], sends_ref[2 * pair + 1 : 2 * pair + 2, :]],
                axis=1,
            ),
            (8, LANES),
        )

    def pack_w(t):
        tables = [hist[t, :, tile(j)] for j in range(tiles)]
        for pair in range(2):
            sendw[t, pair] = pick(tables, sidx[pair], 0)[0:4]

    pack_w(0)

    loads[2].wait()
    loads[3].wait()
    agg = agg_ref[...]
    member = (
        jnp.broadcast_to(agg, (groups, rows)) == lax.broadcasted_iota(jnp.int32, (groups, rows), 0)
    ).astype(jnp.float32)
    counts = jnp.sum(member, axis=1, keepdims=True)
    sizes = jnp.sum(member * counts, axis=0, keepdims=True)
    tent = near_ref[...] * lax.rsqrt(sizes)
    tent_ref[...] = tent
    text[...] = jnp.zeros_like(text)
    for c in range(3):
        text[8 * c : 8 * c + modes, 0:rows] = tent_ref[modes * c : modes * (c + 1), :]
    for pair in range(2):
        for c in range(3):
            sendt[pair, 8 * c : 8 * c + 8, :] = pick(
                [text[8 * c : 8 * c + 8, tile(j)] for j in range(tiles)], sidx[pair], 0
            )

    loads[4].wait()
    loads[5].wait()
    for u, places in enumerate(units):
        if len(places) * places[0][2] < 8:
            cols_u[u] = jnp.zeros((8, LANES), jnp.int32)
        for at, k, count, j in places:
            cols_u[u, at : at + count, :] = cols_ref[k : k + count, tile(j)]

    inverse = invert_rows([diag_ref[p : p + 1, :] for p in range(9)])
    for p in range(9):
        dinv[p : p + 1, :] = inverse[p]
    pl.semaphore_wait(barrier, n_slab * n_sub - 1)
    each_target(functools.partial(w_copy, 0), lambda make, way: make(way).start())
    each_target(t_copy, lambda make, way: make(way).start())
    loads[6].wait()
    for u, places in enumerate(units):
        if len(places) * places[0][2] < 8:
            mats[u] = jnp.zeros(mats.shape[1:], jnp.float32)
        for at, k, count, j in places:
            block = [off_v[p, k : k + count, tile(j)] for p in range(9)]
            for r in range(3):
                scale = [
                    jnp.broadcast_to(dinv[3 * r + q : 3 * r + q + 1, tile(j)], (count, LANES))
                    for q in range(3)
                ]
                for c in range(3):
                    mats[u, 3 * r + c, at : at + count, :] = (
                        scale[0] * block[c] + scale[1] * block[3 + c] + scale[2] * block[6 + c]
                    )

    left = lax.broadcasted_iota(jnp.int32, (8, LANES), 1) < half
    per = -(-len(units) // (ITERS - 1))

    def unit_products(u, unused):
        index = cols_u[u]
        for m in range(modes):
            picked = [
                pick(
                    [
                        jnp.broadcast_to(text[8 * c + m : 8 * c + m + 1, tile(i)], (8, LANES))
                        for i in range(tiles + 2)
                    ],
                    index,
                    0,
                )
                for c in range(3)
            ]
            for r in range(3):
                raw_ref[modes * r + m, u] = (
                    mats[u, 3 * r] * picked[0]
                    + mats[u, 3 * r + 1] * picked[1]
                    + mats[u, 3 * r + 2] * picked[2]
                )
        return unused

    def contribute(tables, first, u):
        index = cols_u[u]
        picked = [pick(tables[c], index, first) for c in range(3)]
        return [sum(mats[u, 3 * r + c] * picked[c] for c in range(3)) for r in range(3)]

    def by_tile(terms):
        whole = [[None] * tiles for r in range(3)]
        for r in range(3):
            for u, places in enumerate(units):
                if len(places) == 1 and places[0][2] == 8:
                    j = places[0][3]
                    old = whole[r][j]
                    whole[r][j] = terms[u][r] if old is None else old + terms[u][r]
            for j in range(tiles):
                old = whole[r][j]
                whole[r][j] = 0.0 if old is None else jnp.sum(old, axis=0, keepdims=True)
            for u, places in enumerate(units):
                if not (len(places) == 1 and places[0][2] == 8):
                    for at, k, count, j in places:
                        whole[r][j] = whole[r][j] + jnp.sum(
                            terms[u][r][at : at + count], axis=0, keepdims=True
                        )
        return whole

    def iterate(t, unused):
        local = [
            [jnp.broadcast_to(hist[t, c : c + 1, tile(i)], (8, LANES)) for i in range(tiles)]
            for c in range(3)
        ]
        inner = by_tile([contribute(local, 0, u) for u in range(len(units))])
        for r in range(3):
            for j in range(tiles):
                hist[t + 1, r : r + 1, tile(j)] = hist[t, r : r + 1, tile(j)] + inner[r][j]

        @pl.when(t == 1)
        def _():
            each_source(t_copy)
            for pair in range(2):
                for c in range(3):
                    text[8 * c : 8 * c + 8, tile(tiles + pair)] = jnp.where(
                        left,
                        recvt[2 * pair, 8 * c : 8 * c + 8, :],
                        recvt[2 * pair + 1, 8 * c : 8 * c + 8, :],
                    )

        lax.fori_loop(
            jnp.clip((t - 1) * per, 0, len(units)), jnp.clip(t * per, 0, len(units)), unit_products, 0
        )
        each_source(functools.partial(w_copy, t))
        merged = [jnp.where(left[0:4], recvw[t, 2 * pair], recvw[t, 2 * pair + 1]) for pair in range(2)]
        ghost = [
            [jnp.broadcast_to(merged[pair][c : c + 1], (8, LANES)) for pair in range(2)]
            for c in range(3)
        ]
        outer = by_tile([contribute(ghost, tiles, u) for u in range(len(units))])
        for r in range(3):
            for j in range(tiles):
                hist[t + 1, r : r + 1, tile(j)] = hist[t + 1, r : r + 1, tile(j)] + outer[r][j]

        @pl.when(t < ITERS - 1)
        def _():
            pack_w(t + 1)
            each_target(functools.partial(w_copy, t + 1), lambda make, way: make(way).start())

        return unused

    lax.fori_loop(0, ITERS, iterate, 0)

    store = pltpu.make_async_copy(raw_ref, raw_hbm, raw_sem)
    store.start()

    def squares(t):
        return jnp.sum(
            sum(hist[t, :, tile(j)] * hist[t, :, tile(j)] for j in range(tiles)), keepdims=True
        )

    lane = lax.broadcasted_iota(jnp.int32, (1, LANES), 1)
    latest = jnp.broadcast_to(squares(ITERS), (1, LANES))
    previous = jnp.broadcast_to(squares(ITERS - 1), (1, LANES))
    own = jnp.where(lane == 0, latest, jnp.where(lane == 1, previous, 0.0))
    me = a * n_sub + b
    devices = n_slab * n_sub
    stat[0] = own

    def stat_copy(step, source):
        target = lax.rem(me + step, devices)
        landing = lax.rem(me + devices - step, devices) if source else me
        return pltpu.make_async_remote_copy(
            src_ref=stat.at[0], dst_ref=stats.at[landing],
            send_sem=ss_sem.at[step], recv_sem=rs_sem.at[landing],
            device_id={"slab": lax.div(target, n_sub), "sub": lax.rem(target, n_sub)},
            device_id_type=MESH,
        )

    def begin(step, unused):
        stat_copy(step, False).start()
        return unused

    def arrive(step, unused):
        stat_copy(step, True).wait_recv()
        return unused

    def sent(step, unused):
        stat_copy(step, False).wait_send()
        return unused

    lax.fori_loop(1, devices, begin, 0)
    stats[me] = own
    lax.fori_loop(1, devices, arrive, 0)
    whole = jnp.sum(stats[...], axis=0)
    latest = whole[:, 0:1]
    previous = whole[:, 1:2]
    rho_ref[...] = jnp.sqrt(latest / (previous + 1e-05))

    lax.fori_loop(1, devices, sent, 0)
    store.wait()
    each_target(t_copy, lambda make, way: make(way).wait_send())

    def drain(t, unused):
        each_target(functools.partial(w_copy, t), lambda make, way: make(way).wait_send())
        return unused

    lax.fori_loop(0, ITERS, drain, 0)


def body(n_slab, n_sub, near_null, aggregates, diag_block, off_blocks, columns, sends, start_vector):
    slots, nine, rows = off_blocks.shape
    wide = rows + 2 * LANES
    count = len(unit_places(slots, rows // LANES))
    f32 = jnp.float32
    vmem = pl.BlockSpec(memory_space=pltpu.VMEM)
    dma = pltpu.SemaphoreType.DMA
    raw, tentative, rho = pl.pallas_call(
        functools.partial(kernel, n_slab, n_sub),
        out_shape=(
            jax.ShapeDtypeStruct((near_null.shape[0], count, 8, LANES), f32),
            jax.ShapeDtypeStruct(near_null.shape, f32),
            jax.ShapeDtypeStruct((1, 1), f32),
        ),
        in_specs=[pl.BlockSpec(memory_space=pl.ANY)] * 7,
        out_specs=(pl.BlockSpec(memory_space=pl.ANY), vmem, vmem),
        scratch_shapes=[
            pltpu.VMEM(near_null.shape, f32),
            pltpu.VMEM((1, rows), jnp.int32),
            pltpu.VMEM(diag_block.shape, f32),
            pltpu.VMEM(columns.shape, jnp.int32),
            pltpu.VMEM(sends.shape, jnp.int32),
            pltpu.VMEM(start_vector.shape, f32),
            pltpu.VMEM((near_null.shape[0], count, 8, LANES), f32),
            pltpu.VMEM((nine, slots, rows), f32),
            pltpu.VMEM((count, 8, LANES), jnp.int32),
            pltpu.VMEM((count, nine, 8, LANES), f32),
            pltpu.VMEM((16, rows), f32),
            pltpu.VMEM((24, wide), f32),
            pltpu.VMEM((ITERS + 1, 8, rows), f32),
            pltpu.VMEM((2, 8, LANES), jnp.int32),
            pltpu.VMEM((ITERS, 2, 4, LANES), f32),
            pltpu.VMEM((ITERS, 4, 4, LANES), f32),
            pltpu.VMEM((2, 24, LANES), f32),
            pltpu.VMEM((4, 24, LANES), f32),
            pltpu.VMEM((1, 1, LANES), f32),
            pltpu.VMEM((n_slab * n_sub, 1, LANES), f32),
            dma((7,)),
            dma,
            dma((ITERS, 4)),
            dma((ITERS, 4)),
            dma((4,)),
            dma((4,)),
            dma((n_slab * n_sub,)),
            dma((n_slab * n_sub,)),
        ],
        compiler_params=pltpu.CompilerParams(collective_id=0, has_side_effects=True),
        name="smooth",
    )(
        near_null, aggregates.reshape(1, rows), diag_block, off_blocks.transpose(1, 0, 2),
        columns, sends, start_vector,
    )
    prolong_off, prolong_self = pl.pallas_call(
        scale_kernel,
        out_shape=(
            jax.ShapeDtypeStruct((near_null.shape[0], slots, rows), jnp.bfloat16),
            jax.ShapeDtypeStruct(near_null.shape, jnp.bfloat16),
        ),
        in_specs=[vmem, vmem, vmem],
        out_specs=(vmem, vmem),
        name="scale",
    )(raw, tentative, rho)
    return (prolong_off.transpose(1, 0, 2), prolong_self, rho.reshape(()))


def solution(mesh):
    placed = (
        P(None, ("slab", "sub")),
        P(("slab", "sub")),
        P(None, ("slab", "sub")),
        P(None, None, ("slab", "sub")),
        P(None, ("slab", "sub")),
        P(None, ("slab", "sub")),
        P(None, ("slab", "sub")),
    )
    return jax.shard_map(
        functools.partial(body, mesh.shape["slab"], mesh.shape["sub"]),
        mesh=mesh,
        in_specs=placed,
        out_specs=(P(None, None, ("slab", "sub")), P(None, ("slab", "sub")), P()),
        check_vma=False,
    )
```

profile of v0, /device:TPU:0, one launch (start us, length us, event | category | flops | bytes accessed | tf_op | source)
XLA Modules:
  0.0 41.4 jit_solution(15429062600698483015)
XLA Ops:
  0.6 36.0 %smooth.1 = (f32[18,13,8,128]{3,2,1,0:T(8,128)}, f32[18,512]{1,0:T(8,128)}, f32[1,1]{1,0:T(1,128)}) custom-call(f32[18,512]{1,0:T(8,128)} %near_hbm.1, s32[1,512]{1,0:T(1,128)} %bitcast.5, f32[9,512]{1,0:T(8,128)} %diag_hbm.1, f32[9,26,512]{2,1,0:T(8,128)} %bitcast.4, s32[26,512]{1,0:T(8,128)} %cols_hbm.1, s32[4,64]{1,0:T(4,128)} %sends_hbm.1, ...), custom_call_target="tpu_custom_call" | custom-call | tf_op jit(solution)/shard_map/smooth/pallas_call | solution.py:392
  36.7 2.9 %scale.1 = (bf16[18,26,512]{2,1,0:T(8,128)(2,1)}, bf16[18,512]{1,0:T(8,128)(2,1)}) custom-call(f32[18,13,8,128]{3,2,1,0:T(8,128)} %get-tuple-element.8.raw_ref, f32[18,512]{1,0:T(8,128)} %get-tuple-element.9.tent_ref, f32[1,1]{1,0:T(1,128)} %get-tuple-element.10.rho_ref), custom_call_target="tpu_custom_call" | custom-call | tf_op jit(solution)/shard_map/scale/pallas_call | solution.py:437
where the time goes:
time: 41.6 us; the launch traced here: 41.4 us
  Pallas kernels  38.9 us (94%)
  between operations  2.46 us (6%)
    pallas_call x1, Pallas kernels, body(): pl.pallas_call(functools.partial(kernel, n_slab, n_sub), out_shape=(jax.S...  36 us
    pallas_call x1, Pallas kernels, body(): pl.pallas_call(scale_kernel, out_shape=(jax.ShapeDtypeStruct((near_null.s...  2.87 us

commit v1 on v0

--- a/solution.py
+++ b/solution.py
@@ -66,8 +66,9 @@
     return units
 
 
-def scale_kernel(raw_ref, tent_ref, rho_ref, off_ref, self_ref):
+def scale_kernel(raw_ref, tent_ref, rho_ref, off_ref, self_ref, out_rho_ref):
     slots, rows = off_ref.shape[1:]
+    out_rho_ref[...] = rho_ref[...]
     inverse = OMEGA / rho_ref[...]
     factor = jnp.broadcast_to(-inverse, (8, LANES))
     places = unit_places(slots, rows // LANES)
@@ -86,10 +87,10 @@
 def kernel(
     n_slab, n_sub,
     near_hbm, agg_hbm, diag_hbm, off_hbm, cols_hbm, sends_hbm, start_hbm,
-    raw_hbm, tent_ref, rho_ref,
-    near_ref, agg_ref, diag_ref, cols_ref, sends_ref, start_ref, raw_ref, off_v, cols_u, mats, dinv, text, hist, sidx,
+    raw_ref, tent_ref, rho_ref,
+    near_ref, agg_ref, diag_ref, cols_ref, sends_ref, start_ref, off_v, cols_u, mats, dinv, text, hist, sidx,
     sendw, recvw, sendt, recvt, stat, stats,
-    off_sem, raw_sem, sendw_sem, recvw_sem, sendt_sem, recvt_sem,
+    off_sem, sendw_sem, recvw_sem, sendt_sem, recvt_sem,
     ss_sem, rs_sem,
 ):
     slots, rows = cols_ref.shape
@@ -325,8 +326,6 @@
 
     lax.fori_loop(0, ITERS, iterate, 0)
 
-    store = pltpu.make_async_copy(raw_ref, raw_hbm, raw_sem)
-    store.start()
 
     def squares(t):
         return jnp.sum(
@@ -372,7 +371,6 @@
     rho_ref[...] = jnp.sqrt(latest / (previous + 1e-05))
 
     lax.fori_loop(1, devices, sent, 0)
-    store.wait()
     each_target(t_copy, lambda make, way: make(way).wait_send())
 
     def drain(t, unused):
@@ -392,12 +390,12 @@
     raw, tentative, rho = pl.pallas_call(
         functools.partial(kernel, n_slab, n_sub),
         out_shape=(
-            jax.ShapeDtypeStruct((near_null.shape[0], count, 8, LANES), f32),
-            jax.ShapeDtypeStruct(near_null.shape, f32),
+            pltpu.VMEM((near_null.shape[0], count, 8, LANES), f32),
+            pltpu.VMEM(near_null.shape, f32),
             jax.ShapeDtypeStruct((1, 1), f32),
         ),
-        in_specs=[pl.BlockSpec(memory_space=pl.ANY)] * 7,
-        out_specs=(pl.BlockSpec(memory_space=pl.ANY), vmem, vmem),
+        in_specs=[pl.BlockSpec(memory_space=pltpu.HBM)] * 7,
+        out_specs=(vmem, vmem, vmem),
         scratch_shapes=[
             pltpu.VMEM(near_null.shape, f32),
             pltpu.VMEM((1, rows), jnp.int32),
@@ -405,7 +403,6 @@
             pltpu.VMEM(columns.shape, jnp.int32),
             pltpu.VMEM(sends.shape, jnp.int32),
             pltpu.VMEM(start_vector.shape, f32),
-            pltpu.VMEM((near_null.shape[0], count, 8, LANES), f32),
             pltpu.VMEM((nine, slots, rows), f32),
             pltpu.VMEM((count, 8, LANES), jnp.int32),
             pltpu.VMEM((count, nine, 8, LANES), f32),
@@ -420,7 +417,6 @@
             pltpu.VMEM((1, 1, LANES), f32),
             pltpu.VMEM((n_slab * n_sub, 1, LANES), f32),
             dma((7,)),
-            dma,
             dma((ITERS, 4)),
             dma((ITERS, 4)),
             dma((4,)),
@@ -428,20 +424,27 @@
             dma((n_slab * n_sub,)),
             dma((n_slab * n_sub,)),
         ],
-        compiler_params=pltpu.CompilerParams(collective_id=0, has_side_effects=True),
+        compiler_params=pltpu.CompilerParams(collective_id=0, has_side_effects=True, vmem_limit_bytes=16777216),
         name="smooth",
     )(
-        near_null, aggregates.reshape(1, rows), diag_block, off_blocks.transpose(1, 0, 2),
-        columns, sends, start_vector,
+        *[
+            pltpu.with_memory_space_constraint(x, pltpu.HBM)
+            for x in (
+                near_null, aggregates.reshape(1, rows), diag_block, off_blocks.transpose(1, 0, 2),
+                columns, sends, start_vector,
+            )
+        ]
     )
-    prolong_off, prolong_self = pl.pallas_call(
+    prolong_off, prolong_self, rho = pl.pallas_call(
         scale_kernel,
         out_shape=(
             jax.ShapeDtypeStruct((near_null.shape[0], slots, rows), jnp.bfloat16),
             jax.ShapeDtypeStruct(near_null.shape, jnp.bfloat16),
+            jax.ShapeDtypeStruct((1, 1), f32),
         ),
         in_specs=[vmem, vmem, vmem],
-        out_specs=(vmem, vmem),
+        out_specs=(vmem, vmem, vmem),
+        compiler_params=pltpu.CompilerParams(vmem_limit_bytes=16777216),
         name="scale",
     )(raw, tentative, rho)
     return (prolong_off.transpose(1, 0, 2), prolong_self, rho.reshape(()))

time: 41.6 us -> 38.4 us (0.923)
  between operations: 2.46 us -> 0.64 us
  Pallas kernels: 38.9 us -> 37.6 us
    pallas_call x1, Pallas kernels: 2.87 us -> 1.63 us  [body(): pl.pallas_call(scale_kernel, out_shape=(jax.ShapeDtypeStruct((near_null.s...]
where the time goes in v1:
time: 38.4 us; the launch traced here: 38.2 us
  Pallas kernels  37.6 us (98%)
  between operations  0.64 us (2%)
    pallas_call x1, Pallas kernels, body(): pl.pallas_call(functools.partial(kernel, n_slab, n_sub), out_shape=(pltpu...  35.9 us
    pallas_call x1, Pallas kernels, body(): pl.pallas_call(scale_kernel, out_shape=(jax.ShapeDtypeStruct((near_null.s...  1.63 us

profile of v1, /device:TPU:0, one launch (start us, length us, event | category | flops | bytes accessed | tf_op | source)
XLA Modules:
  0.0 38.2 jit_solution(148509262274192677)
XLA Ops:
  0.6 35.9 %smooth.1 = (f32[18,13,8,128]{3,2,1,0:T(8,128)S(1)}, f32[18,512]{1,0:T(8,128)S(1)}, f32[1,1]{1,0:T(1,128)}) custom-call(f32[18,512]{1,0:T(8,128)} %near_hbm.1, s32[1,512]{1,0:T(1,128)} %bitcast.5, f32[9,512]{1,0:T(8,128)} %diag_hbm.1, f32[9,26,512]{2,1,0:T(8,128)} %bitcast.4, s32[26,512]{1,0:T(8,128)} %cols_hbm.1, s32[4,64]{1,0:T(4,128)} %sends_hbm.1, ...), custom_call_target="tpu_custom_call" | custom-call | tf_op jit(solution)/shard_map/smooth/pallas_call | solution.py:390
  36.6 1.6 %scale.1 = (bf16[18,26,512]{2,1,0:T(8,128)(2,1)}, bf16[18,512]{1,0:T(8,128)(2,1)}, f32[1,1]{1,0:T(1,128)}) custom-call(f32[18,13,8,128]{3,2,1,0:T(8,128)S(1)} %get-tuple-element.9.raw_ref, f32[18,512]{1,0:T(8,128)S(1)} %get-tuple-element.10.tent_ref, f32[1,1]{1,0:T(1,128)} %get-tuple-element.11.rho_ref), custom_call_target="tpu_custom_call" | custom-call | tf_op jit(solution)/shard_map/scale/pallas_call | solution.py:438

commit v2 on v1

--- a/solution.py
+++ b/solution.py
@@ -11,6 +11,9 @@
 OMEGA = 4.0 / 3.0
 LANES = 128
 MESH = pl.DeviceIdType.MESH
+CIRCLE = [
+    (x, y) for x in range(-2, 3) for y in range(-2, 3) if 1 <= abs(x) + abs(y) <= 2
+]
 
 
 def lane_gather(table, lanes):
@@ -122,16 +125,27 @@
     recvt[...] = jnp.zeros_like(recvt)
     barrier = pltpu.get_barrier_semaphore()
 
-    def greet(step, unused):
+    def present(x, y):
+        return (a + x >= 0) & (a + x < n_slab) & (b + y >= 0) & (b + y < n_sub)
+
+    def greet(x, y):
+        pl.semaphore_signal(
+            barrier, inc=1, device_id={"slab": a + x, "sub": b + y}, device_id_type=MESH
+        )
+
+    def greet_any(step, unused):
         target = lax.rem(a * n_sub + b + step, n_slab * n_sub)
-        pl.semaphore_signal(
-            barrier, inc=1,
-            device_id={"slab": lax.div(target, n_sub), "sub": lax.rem(target, n_sub)},
-            device_id_type=MESH,
-        )
-        return unused
-
-    lax.fori_loop(1, n_slab * n_sub, greet, 0)
+        greet(lax.div(target, n_sub) - a, lax.rem(target, n_sub) - b)
+        return unused
+
+    near = n_slab - 1 + n_sub - 1 <= ITERS + 2
+    if near:
+        for x, y in CIRCLE:
+            pl.when(present(x, y))(functools.partial(greet, x, y))
+        greeters = sum(present(x, y).astype(jnp.int32) for x, y in CIRCLE)
+    else:
+        lax.fori_loop(1, n_slab * n_sub, greet_any, 0)
+        greeters = n_slab * n_sub - 1
 
     ways = (
         ("sub", b + 1, 0, b < n_sub - 1, b > 0),
@@ -214,7 +228,7 @@
     inverse = invert_rows([diag_ref[p : p + 1, :] for p in range(9)])
     for p in range(9):
         dinv[p : p + 1, :] = inverse[p]
-    pl.semaphore_wait(barrier, n_slab * n_sub - 1)
+    pl.semaphore_wait(barrier, greeters)
     each_target(functools.partial(w_copy, 0), lambda make, way: make(way).start())
     each_target(t_copy, lambda make, way: make(way).start())
     loads[6].wait()

time: 38.4 us -> 37.9 us (0.987)
  Pallas kernels: 37.6 us -> 37.1 us
    pallas_call x1, Pallas kernels: 35.9 us -> 35.5 us  [body(): pl.pallas_call(functools.partial(kernel, n_slab, n_sub), out_shape=(pltpu...]
where the time goes in v2:
time: 37.9 us; the launch traced here: 37.7 us
  Pallas kernels  37.1 us (98%)
  between operations  0.64 us (2%)
    pallas_call x1, Pallas kernels, body(): pl.pallas_call(functools.partial(kernel, n_slab, n_sub), out_shape=(pltpu...  35.5 us
    pallas_call x1, Pallas kernels, body(): pl.pallas_call(scale_kernel, out_shape=(jax.ShapeDtypeStruct((near_null.s...  1.63 us

profile of v2, /device:TPU:0, one launch (start us, length us, event | category | flops | bytes accessed | tf_op | source)
XLA Modules:
  0.0 37.7 jit_solution(6164718317666313410)
XLA Ops:
  0.6 35.5 %smooth.1 = (f32[18,13,8,128]{3,2,1,0:T(8,128)S(1)}, f32[18,512]{1,0:T(8,128)S(1)}, f32[1,1]{1,0:T(1,128)}) custom-call(f32[18,512]{1,0:T(8,128)} %near_hbm.1, s32[1,512]{1,0:T(1,128)} %bitcast.5, f32[9,512]{1,0:T(8,128)} %diag_hbm.1, f32[9,26,512]{2,1,0:T(8,128)} %bitcast.4, s32[26,512]{1,0:T(8,128)} %cols_hbm.1, s32[4,64]{1,0:T(4,128)} %sends_hbm.1, ...), custom_call_target="tpu_custom_call" | custom-call | tf_op jit(solution)/shard_map/smooth/pallas_call | solution.py:404
  36.1 1.6 %scale.1 = (bf16[18,26,512]{2,1,0:T(8,128)(2,1)}, bf16[18,512]{1,0:T(8,128)(2,1)}, f32[1,1]{1,0:T(1,128)}) custom-call(f32[18,13,8,128]{3,2,1,0:T(8,128)S(1)} %get-tuple-element.9.raw_ref, f32[18,512]{1,0:T(8,128)S(1)} %get-tuple-element.10.tent_ref, f32[1,1]{1,0:T(1,128)} %get-tuple-element.11.rho_ref), custom_call_target="tpu_custom_call" | custom-call | tf_op jit(solution)/shard_map/scale/pallas_call | solution.py:452

commit v3 on v2

--- a/solution.py
+++ b/solution.py
@@ -11,9 +11,12 @@
 OMEGA = 4.0 / 3.0
 LANES = 128
 MESH = pl.DeviceIdType.MESH
-CIRCLE = [
-    (x, y) for x in range(-2, 3) for y in range(-2, 3) if 1 <= abs(x) + abs(y) <= 2
-]
+DEPTH = 2
+BLOCKS = ITERS // DEPTH
+WAYS = [(0, 1), (0, -1), (1, 0), (-1, 0)]
+FAR = [(-1, -1), (-1, 1), (1, -1), (1, 1), (-2, 0), (2, 0), (0, -2), (0, 2)]
+CIRCLE = WAYS + FAR
+ORDER = list(range(len(WAYS), len(CIRCLE))) + list(range(len(WAYS)))
 
 
 def lane_gather(table, lanes):
@@ -91,17 +94,19 @@
     n_slab, n_sub,
     near_hbm, agg_hbm, diag_hbm, off_hbm, cols_hbm, sends_hbm, start_hbm,
     raw_ref, tent_ref, rho_ref,
-    near_ref, agg_ref, diag_ref, cols_ref, sends_ref, start_ref, off_v, cols_u, mats, dinv, text, hist, sidx,
-    sendw, recvw, sendt, recvt, stat, stats,
-    off_sem, sendw_sem, recvw_sem, sendt_sem, recvt_sem,
+    near_ref, agg_ref, diag_ref, cols_ref, sends_ref, start_ref, off_v, cols_u, mats, rest_m, dinv, text, hist, sidx,
+    sendw, recvw, recvp, sendg, recvg, gcol, sendt, recvt, stat, stats,
+    off_sem, sendw_sem, recvw_sem, sendg_sem, recvg_sem, sendt_sem, recvt_sem,
     ss_sem, rs_sem,
 ):
     slots, rows = cols_ref.shape
     half = sends_ref.shape[1]
     tiles = rows // LANES
     units = unit_places(slots, tiles)
+    groups = -(-slots // 8)
+    gunits, planes = sendg.shape[1:3]
     modes = near_ref.shape[0] // 3
-    groups = rows // 8
+    sizes_of = rows // 8
     a = lax.axis_index("slab")
     b = lax.axis_index("sub")
     loads = [
@@ -121,8 +126,6 @@
     for load in loads:
         load.start()
 
-    recvw[...] = jnp.zeros_like(recvw)
-    recvt[...] = jnp.zeros_like(recvt)
     barrier = pltpu.get_barrier_semaphore()
 
     def present(x, y):
@@ -147,36 +150,53 @@
         lax.fori_loop(1, n_slab * n_sub, greet_any, 0)
         greeters = n_slab * n_sub - 1
 
-    ways = (
-        ("sub", b + 1, 0, b < n_sub - 1, b > 0),
-        ("sub", b - 1, 0, b > 0, b < n_sub - 1),
-        ("slab", a + 1, 1, a < n_slab - 1, a > 0),
-        ("slab", a - 1, 1, a > 0, a < n_slab - 1),
-    )
-
-    def w_copy(t, way):
-        axis, target, pair, unused, unused2 = ways[way]
+    def clear(place):
+        if place < len(WAYS):
+            for ref in (recvw.at[:, place], recvg.at[place], recvt.at[place]):
+                ref[...] = jnp.zeros(ref.shape, jnp.float32)
+        else:
+            ref = recvp.at[:, place - len(WAYS)]
+            ref[...] = jnp.zeros(ref.shape, jnp.float32)
+
+    for place, (x, y) in enumerate(CIRCLE):
+        pl.when(jnp.logical_not(present(-x, -y)))(functools.partial(clear, place))
+
+    def remote(source, target, sent, came, place):
+        x, y = CIRCLE[place]
         return pltpu.make_async_remote_copy(
-            src_ref=sendw.at[t, pair], dst_ref=recvw.at[t, way],
-            send_sem=sendw_sem.at[t, way], recv_sem=recvw_sem.at[t, way],
-            device_id={axis: target}, device_id_type=MESH,
+            src_ref=source, dst_ref=target, send_sem=sent, recv_sem=came,
+            device_id={"slab": a + x, "sub": b + y}, device_id_type=MESH,
         )
 
+    def w_copy(turn, place):
+        if place < len(WAYS):
+            source, target = sendw.at[turn], recvw.at[turn, place]
+        else:
+            source, target = sendw.at[turn, 0], recvp.at[turn, place - len(WAYS)]
+        return remote(source, target, sendw_sem.at[turn, place], recvw_sem.at[turn, place], place)
+
+    def g_copy(way):
+        return remote(sendg.at[way], recvg.at[way], sendg_sem.at[way], recvg_sem.at[way], way)
+
     def t_copy(way):
-        axis, target, pair, unused, unused2 = ways[way]
-        return pltpu.make_async_remote_copy(
-            src_ref=sendt.at[pair], dst_ref=recvt.at[way],
-            send_sem=sendt_sem.at[way], recv_sem=recvt_sem.at[way],
-            device_id={axis: target}, device_id_type=MESH,
-        )
-
-    def each_target(make, act):
-        for way in range(4):
-            pl.when(ways[way][3])(functools.partial(act, make, way))
-
-    def each_source(make):
-        for way in range(4):
-            pl.when(ways[way][4])(functools.partial(lambda way: make(way).wait_recv(), way))
+        return remote(sendt.at[way // 2], recvt.at[way], sendt_sem.at[way], recvt_sem.at[way], way)
+
+    def each_target(make, places, act):
+        for place in places:
+            x, y = CIRCLE[place]
+            pl.when(present(x, y))(functools.partial(lambda place: act(make(place)), place))
+
+    def each_source(make, places):
+        for place in places:
+            x, y = CIRCLE[place]
+            pl.when(present(-x, -y))(functools.partial(lambda place: make(place).wait_recv(), place))
+
+    def begin_copy(copy):
+        copy.start()
+
+    ways = range(len(WAYS))
+    far = range(len(WAYS), len(CIRCLE))
+    left = lax.broadcasted_iota(jnp.int32, (8, LANES), 1) < half
 
     hist[...] = jnp.zeros_like(hist)
     loads[0].wait()
@@ -191,18 +211,20 @@
             (8, LANES),
         )
 
-    def pack_w(t):
-        tables = [hist[t, :, tile(j)] for j in range(tiles)]
-        for pair in range(2):
-            sendw[t, pair] = pick(tables, sidx[pair], 0)[0:4]
-
-    pack_w(0)
+    def pack_w(turn, step):
+        tables = [hist[step, :, tile(j)] for j in range(tiles)]
+        picked = [pick(tables, sidx[pair], 0) for pair in range(2)]
+        sendw[turn, 0] = jnp.concatenate([picked[0][0:4], picked[1][0:4]], axis=0)
+        for j in range(0, tiles, 2):
+            sendw[turn, 1 + j // 2] = jnp.concatenate([tables[j][0:4], tables[j + 1][0:4]], axis=0)
+
+    pack_w(0, 0)
 
     loads[2].wait()
     loads[3].wait()
     agg = agg_ref[...]
     member = (
-        jnp.broadcast_to(agg, (groups, rows)) == lax.broadcasted_iota(jnp.int32, (groups, rows), 0)
+        jnp.broadcast_to(agg, (sizes_of, rows)) == lax.broadcasted_iota(jnp.int32, (sizes_of, rows), 0)
     ).astype(jnp.float32)
     counts = jnp.sum(member, axis=1, keepdims=True)
     sizes = jnp.sum(member * counts, axis=0, keepdims=True)
@@ -219,18 +241,20 @@
 
     loads[4].wait()
     loads[5].wait()
+    rest_m[...] = jnp.zeros_like(rest_m)
     for u, places in enumerate(units):
         if len(places) * places[0][2] < 8:
             cols_u[u] = jnp.zeros((8, LANES), jnp.int32)
         for at, k, count, j in places:
             cols_u[u, at : at + count, :] = cols_ref[k : k + count, tile(j)]
+            if count < 8:
+                rest_m[planes - 1, j, 0:count, :] = cols_ref[k : k + count, tile(j)].astype(jnp.float32)
 
     inverse = invert_rows([diag_ref[p : p + 1, :] for p in range(9)])
     for p in range(9):
         dinv[p : p + 1, :] = inverse[p]
     pl.semaphore_wait(barrier, greeters)
-    each_target(functools.partial(w_copy, 0), lambda make, way: make(way).start())
-    each_target(t_copy, lambda make, way: make(way).start())
+    each_target(functools.partial(w_copy, 0), ORDER, begin_copy)
     loads[6].wait()
     for u, places in enumerate(units):
         if len(places) * places[0][2] < 8:
@@ -243,12 +267,36 @@
                     for q in range(3)
                 ]
                 for c in range(3):
-                    mats[u, 3 * r + c, at : at + count, :] = (
-                        scale[0] * block[c] + scale[1] * block[3 + c] + scale[2] * block[6 + c]
-                    )
-
-    left = lax.broadcasted_iota(jnp.int32, (8, LANES), 1) < half
-    per = -(-len(units) // (ITERS - 1))
+                    entry = scale[0] * block[c] + scale[1] * block[3 + c] + scale[2] * block[6 + c]
+                    mats[u, 3 * r + c, at : at + count, :] = entry
+                    if count < 8:
+                        rest_m[3 * r + c, j, 0:count, :] = entry
+
+    def source(q, group, j):
+        if 8 * (group + 1) > slots:
+            return rest_m[q, j]
+        u = group * tiles + j
+        return cols_u[u].astype(jnp.float32) if q == planes - 1 else mats[u, q]
+
+    def chosen(q, group, pair):
+        if group >= groups:
+            return jnp.zeros((8, LANES), jnp.float32)
+        return pick([source(q, group, j) for j in range(tiles)], sidx[pair], 0)
+
+    for pair in range(2):
+        for v in range(gunits):
+            for q in range(planes):
+                low = chosen(q, 2 * v, pair)
+                high = chosen(q, 2 * v + 1, pair)
+                sendg[2 * pair, v, q] = jnp.where(left, low, pltpu.roll(high, half, 1))
+                sendg[2 * pair + 1, v, q] = jnp.where(left, pltpu.roll(low, half, 1), high)
+        each_target(g_copy, (2 * pair, 2 * pair + 1), begin_copy)
+    each_target(t_copy, ways, begin_copy)
+
+    per = -(-len(units) // (BLOCKS - 1))
+
+    def spread(row):
+        return jnp.broadcast_to(row, (8, LANES))
 
     def unit_products(u, unused):
         index = cols_u[u]
@@ -256,7 +304,7 @@
             picked = [
                 pick(
                     [
-                        jnp.broadcast_to(text[8 * c + m : 8 * c + m + 1, tile(i)], (8, LANES))
+                        spread(text[8 * c + m : 8 * c + m + 1, tile(i)])
                         for i in range(tiles + 2)
                     ],
                     index,
@@ -276,6 +324,16 @@
         index = cols_u[u]
         picked = [pick(tables[c], index, first) for c in range(3)]
         return [sum(mats[u, 3 * r + c] * picked[c] for c in range(3)) for r in range(3)]
+
+    def contribute_near(tables, first, way):
+        total = [None] * 3
+        for v in range(gunits):
+            index = gcol[way, v]
+            picked = [pick(tables[c], index, first) for c in range(3)]
+            for r in range(3):
+                term = sum(recvg[way, v, 3 * r + c] * picked[c] for c in range(3))
+                total[r] = term if total[r] is None else total[r] + term
+        return total
 
     def by_tile(terms):
         whole = [[None] * tiles for r in range(3)]
@@ -296,19 +354,30 @@
                         )
         return whole
 
-    def iterate(t, unused):
-        local = [
-            [jnp.broadcast_to(hist[t, c : c + 1, tile(i)], (8, LANES)) for i in range(tiles)]
-            for c in range(3)
-        ]
-        inner = by_tile([contribute(local, 0, u) for u in range(len(units))])
+    def own_part(step):
+        tables = [[spread(hist[step, c : c + 1, tile(i)]) for i in range(tiles)] for c in range(3)]
+        inner = by_tile([contribute(tables, 0, u) for u in range(len(units))])
         for r in range(3):
             for j in range(tiles):
-                hist[t + 1, r : r + 1, tile(j)] = hist[t, r : r + 1, tile(j)] + inner[r][j]
-
-        @pl.when(t == 1)
+                hist[step + 1, r : r + 1, tile(j)] = hist[step, r : r + 1, tile(j)] + inner[r][j]
+
+    def ghost_part(step, tables):
+        outer = by_tile([contribute(tables, tiles, u) for u in range(len(units))])
+        for r in range(3):
+            for j in range(tiles):
+                hist[step + 1, r : r + 1, tile(j)] = hist[step + 1, r : r + 1, tile(j)] + outer[r][j]
+
+    def halves(first, second, pair):
+        both = jnp.where(left, first, second)
+        return [both[4 * pair + c : 4 * pair + c + 1] for c in range(3)]
+
+    def iterate(turn, unused):
+        step = DEPTH * turn
+        own_part(step)
+
+        @pl.when(turn == 1)
         def _():
-            each_source(t_copy)
+            each_source(t_copy, ways)
             for pair in range(2):
                 for c in range(3):
                     text[8 * c : 8 * c + 8, tile(tiles + pair)] = jnp.where(
@@ -318,28 +387,66 @@
                     )
 
         lax.fori_loop(
-            jnp.clip((t - 1) * per, 0, len(units)), jnp.clip(t * per, 0, len(units)), unit_products, 0
+            jnp.clip((turn - 1) * per, 0, len(units)), jnp.clip(turn * per, 0, len(units)), unit_products, 0
         )
-        each_source(functools.partial(w_copy, t))
-        merged = [jnp.where(left[0:4], recvw[t, 2 * pair], recvw[t, 2 * pair + 1]) for pair in range(2)]
-        ghost = [
-            [jnp.broadcast_to(merged[pair][c : c + 1], (8, LANES)) for pair in range(2)]
-            for c in range(3)
+        each_source(functools.partial(w_copy, turn), ways)
+        merged = [
+            halves(recvw[turn, 2 * pair, 0], recvw[turn, 2 * pair + 1, 0], pair) for pair in range(2)
         ]
-        outer = by_tile([contribute(ghost, tiles, u) for u in range(len(units))])
+        ghost_part(step, [[spread(merged[pair][c]) for pair in range(2)] for c in range(3)])
+
+        @pl.when(turn == 0)
+        def _():
+            each_source(g_copy, ways)
+            for way in ways:
+                for v in range(gunits):
+                    gcol[way, v] = recvg[way, v, planes - 1].astype(jnp.int32)
+
+        inside = []
+        for way in ways:
+            tables = [
+                [
+                    spread(recvw[turn, way, 1 + i // 2, 4 * (i % 2) + c : 4 * (i % 2) + c + 1, :])
+                    for i in range(tiles)
+                ]
+                for c in range(3)
+            ]
+            inside.append(contribute_near(tables, 0, way))
+        own_part(step + 1)
+
+        each_source(functools.partial(w_copy, turn), far)
+
+        def packed(way, other):
+            x, y = (WAYS[way][axis] + WAYS[other][axis] for axis in range(2))
+            return sendw[turn, 0] if (x, y) == (0, 0) else recvp[turn, FAR.index((x, y))]
+
+        total = []
+        for way in ways:
+            rows_of = [
+                halves(packed(way, 2 * pair), packed(way, 2 * pair + 1), pair) for pair in range(2)
+            ]
+            outside = contribute_near(
+                [[spread(rows_of[pair][c]) for pair in range(2)] for c in range(3)], tiles, way
+            )
+            total.append([inside[way][r] + outside[r] for r in range(3)])
+        later = [[], [], []]
         for r in range(3):
-            for j in range(tiles):
-                hist[t + 1, r : r + 1, tile(j)] = hist[t + 1, r : r + 1, tile(j)] + outer[r][j]
-
-        @pl.when(t < ITERS - 1)
+            for pair in range(2):
+                first, second = total[2 * pair][r], total[2 * pair + 1][r]
+                both = jnp.where(left, first, second) + pltpu.roll(
+                    jnp.where(left, second, first), half, 1
+                )
+                later[r].append(spread(merged[pair][r] + jnp.sum(both, axis=0, keepdims=True)))
+        ghost_part(step + 1, later)
+
+        @pl.when(turn < BLOCKS - 1)
         def _():
-            pack_w(t + 1)
-            each_target(functools.partial(w_copy, t + 1), lambda make, way: make(way).start())
+            pack_w(turn + 1, step + DEPTH)
+            each_target(functools.partial(w_copy, turn + 1), ORDER, begin_copy)
 
         return unused
 
-    lax.fori_loop(0, ITERS, iterate, 0)
-
+    lax.fori_loop(0, BLOCKS, iterate, 0)
 
     def squares(t):
         return jnp.sum(
@@ -385,19 +492,25 @@
     rho_ref[...] = jnp.sqrt(latest / (previous + 1e-05))
 
     lax.fori_loop(1, devices, sent, 0)
-    each_target(t_copy, lambda make, way: make(way).wait_send())
-
-    def drain(t, unused):
-        each_target(functools.partial(w_copy, t), lambda make, way: make(way).wait_send())
+    def settle(copy):
+        copy.wait_send()
+
+    each_target(g_copy, ways, settle)
+    each_target(t_copy, ways, settle)
+
+    def drain(turn, unused):
+        each_target(functools.partial(w_copy, turn), ORDER, settle)
         return unused
 
-    lax.fori_loop(0, ITERS, drain, 0)
+    lax.fori_loop(0, BLOCKS, drain, 0)
 
 
 def body(n_slab, n_sub, near_null, aggregates, diag_block, off_blocks, columns, sends, start_vector):
     slots, nine, rows = off_blocks.shape
     wide = rows + 2 * LANES
     count = len(unit_places(slots, rows // LANES))
+    parts = 1 + rows // (2 * LANES)
+    gunits = -(-slots // 16)
     f32 = jnp.float32
     vmem = pl.BlockSpec(memory_space=pltpu.VMEM)
     dma = pltpu.SemaphoreType.DMA
@@ -420,19 +533,26 @@
             pltpu.VMEM((nine, slots, rows), f32),
             pltpu.VMEM((count, 8, LANES), jnp.int32),
             pltpu.VMEM((count, nine, 8, LANES), f32),
+            pltpu.VMEM((nine + 1, rows // LANES, 8, LANES), f32),
             pltpu.VMEM((16, rows), f32),
             pltpu.VMEM((24, wide), f32),
             pltpu.VMEM((ITERS + 1, 8, rows), f32),
             pltpu.VMEM((2, 8, LANES), jnp.int32),
-            pltpu.VMEM((ITERS, 2, 4, LANES), f32),
-            pltpu.VMEM((ITERS, 4, 4, LANES), f32),
+            pltpu.VMEM((BLOCKS, parts, 8, LANES), f32),
+            pltpu.VMEM((BLOCKS, len(WAYS), parts, 8, LANES), f32),
+            pltpu.VMEM((BLOCKS, len(FAR), 8, LANES), f32),
+            pltpu.VMEM((len(WAYS), gunits, nine + 1, 8, LANES), f32),
+            pltpu.VMEM((len(WAYS), gunits, nine + 1, 8, LANES), f32),
+            pltpu.VMEM((len(WAYS), gunits, 8, LANES), jnp.int32),
             pltpu.VMEM((2, 24, LANES), f32),
             pltpu.VMEM((4, 24, LANES), f32),
             pltpu.VMEM((1, 1, LANES), f32),
             pltpu.VMEM((n_slab * n_sub, 1, LANES), f32),
             dma((7,)),
-            dma((ITERS, 4)),
-            dma((ITERS, 4)),
+            dma((BLOCKS, len(CIRCLE))),
+            dma((BLOCKS, len(CIRCLE))),
+            dma((4,)),
+            dma((4,)),
             dma((4,)),
             dma((4,)),
             dma((n_slab * n_sub,)),

time: 37.9 us -> 34.5 us (0.910)
  Pallas kernels: 37.1 us -> 33.7 us
    pallas_call x1, Pallas kernels: 35.5 us -> 32 us  [body(): pl.pallas_call(functools.partial(kernel, n_slab, n_sub), out_shape=(pltpu...]
where the time goes in v3:
time: 34.5 us; the launch traced here: 34.3 us
  Pallas kernels  33.7 us (98%)
  between operations  0.64 us (2%)
    pallas_call x1, Pallas kernels, body(): pl.pallas_call(functools.partial(kernel, n_slab, n_sub), out_shape=(pltpu...  32 us
    pallas_call x1, Pallas kernels, body(): pl.pallas_call(scale_kernel, out_shape=(jax.ShapeDtypeStruct((near_null.s...  1.63 us

profile of v3, /device:TPU:0, one launch (start us, length us, event | category | flops | bytes accessed | tf_op | source)
XLA Modules:
  0.0 34.3 jit_solution(10905805801051708325)
XLA Ops:
  0.6 32.0 %smooth.1 = (f32[18,13,8,128]{3,2,1,0:T(8,128)S(1)}, f32[18,512]{1,0:T(8,128)S(1)}, f32[1,1]{1,0:T(1,128)}) custom-call(f32[18,512]{1,0:T(8,128)} %near_hbm.1, s32[1,512]{1,0:T(1,128)} %bitcast.5, f32[9,512]{1,0:T(8,128)} %diag_hbm.1, f32[9,26,512]{2,1,0:T(8,128)} %bitcast.4, s32[26,512]{1,0:T(8,128)} %cols_hbm.1, s32[4,64]{1,0:T(4,128)} %sends_hbm.1, ...), custom_call_target="tpu_custom_call" | custom-call | tf_op jit(solution)/shard_map/smooth/pallas_call | solution.py:517
  32.7 1.6 %scale.1 = (bf16[18,26,512]{2,1,0:T(8,128)(2,1)}, bf16[18,512]{1,0:T(8,128)(2,1)}, f32[1,1]{1,0:T(1,128)}) custom-call(f32[18,13,8,128]{3,2,1,0:T(8,128)S(1)} %get-tuple-element.9.raw_ref, f32[18,512]{1,0:T(8,128)S(1)} %get-tuple-element.10.tent_ref, f32[1,1]{1,0:T(1,128)} %get-tuple-element.11.rho_ref), custom_call_target="tpu_custom_call" | custom-call | tf_op jit(solution)/shard_map/scale/pallas_call | solution.py:572

commit v4 on v3

--- a/solution.py
+++ b/solution.py
@@ -11,6 +11,7 @@
 OMEGA = 4.0 / 3.0
 LANES = 128
 MESH = pl.DeviceIdType.MESH
+LOAD_ORDER = [0, 1, 4, 5, 2, 3]
 DEPTH = 2
 BLOCKS = ITERS // DEPTH
 WAYS = [(0, 1), (0, -1), (1, 0), (-1, 0)]
@@ -95,8 +96,8 @@
     near_hbm, agg_hbm, diag_hbm, off_hbm, cols_hbm, sends_hbm, start_hbm,
     raw_ref, tent_ref, rho_ref,
     near_ref, agg_ref, diag_ref, cols_ref, sends_ref, start_ref, off_v, cols_u, mats, rest_m, dinv, text, hist, sidx,
-    sendw, recvw, recvp, sendg, recvg, gcol, sendt, recvt, stat, stats,
-    off_sem, sendw_sem, recvw_sem, sendg_sem, recvg_sem, sendt_sem, recvt_sem,
+    sendw, recvw, sendu, recvu, sendg, recvg, gcol, sendt, recvt, stat, stats,
+    off_sem, sendw_sem, recvw_sem, sendu_sem, recvu_sem, sendg_sem, recvg_sem, sendt_sem, recvt_sem,
     ss_sem, rs_sem,
 ):
     slots, rows = cols_ref.shape
@@ -109,6 +110,29 @@
     sizes_of = rows // 8
     a = lax.axis_index("slab")
     b = lax.axis_index("sub")
+    barrier = pltpu.get_barrier_semaphore()
+    def present(x, y):
+        return (a + x >= 0) & (a + x < n_slab) & (b + y >= 0) & (b + y < n_sub)
+
+    def greet(x, y):
+        pl.semaphore_signal(
+            barrier, inc=1, device_id={"slab": a + x, "sub": b + y}, device_id_type=MESH
+        )
+
+    def greet_any(step, unused):
+        target = lax.rem(a * n_sub + b + step, n_slab * n_sub)
+        greet(lax.div(target, n_sub) - a, lax.rem(target, n_sub) - b)
+        return unused
+
+    near = n_slab - 1 + n_sub - 1 <= ITERS + 2
+    if near:
+        for x, y in CIRCLE:
+            pl.when(present(x, y))(functools.partial(greet, x, y))
+        greeters = sum(present(x, y).astype(jnp.int32) for x, y in CIRCLE)
+    else:
+        lax.fori_loop(1, n_slab * n_sub, greet_any, 0)
+        greeters = n_slab * n_sub - 1
+
     loads = [
         pltpu.make_async_copy(source, target, off_sem.at[number])
         for number, (source, target) in enumerate(
@@ -119,43 +143,24 @@
                 (near_hbm, near_ref),
                 (diag_hbm, diag_ref),
                 (cols_hbm, cols_ref),
-                (off_hbm, off_v),
             )
         )
     ]
-    for load in loads:
-        load.start()
-
-    barrier = pltpu.get_barrier_semaphore()
-
-    def present(x, y):
-        return (a + x >= 0) & (a + x < n_slab) & (b + y >= 0) & (b + y < n_sub)
-
-    def greet(x, y):
-        pl.semaphore_signal(
-            barrier, inc=1, device_id={"slab": a + x, "sub": b + y}, device_id_type=MESH
-        )
-
-    def greet_any(step, unused):
-        target = lax.rem(a * n_sub + b + step, n_slab * n_sub)
-        greet(lax.div(target, n_sub) - a, lax.rem(target, n_sub) - b)
-        return unused
-
-    near = n_slab - 1 + n_sub - 1 <= ITERS + 2
-    if near:
-        for x, y in CIRCLE:
-            pl.when(present(x, y))(functools.partial(greet, x, y))
-        greeters = sum(present(x, y).astype(jnp.int32) for x, y in CIRCLE)
-    else:
-        lax.fori_loop(1, n_slab * n_sub, greet_any, 0)
-        greeters = n_slab * n_sub - 1
+    cuts = [(16 * v, min(16, slots - 16 * v)) for v in range(gunits)]
+    loads += [
+        pltpu.make_async_copy(
+            off_hbm.at[:, pl.ds(k, count)], off_v.at[:, pl.ds(k, count)], off_sem.at[len(loads) + v]
+        )
+        for v, (k, count) in enumerate(cuts)
+    ]
+    for number in LOAD_ORDER + list(range(len(LOAD_ORDER), len(loads))):
+        loads[number].start()
 
     def clear(place):
+        cleared = [recvw.at[:, place]]
         if place < len(WAYS):
-            for ref in (recvw.at[:, place], recvg.at[place], recvt.at[place]):
-                ref[...] = jnp.zeros(ref.shape, jnp.float32)
-        else:
-            ref = recvp.at[:, place - len(WAYS)]
+            cleared += [recvu.at[:, place], recvg.at[place], recvt.at[place]]
+        for ref in cleared:
             ref[...] = jnp.zeros(ref.shape, jnp.float32)
 
     for place, (x, y) in enumerate(CIRCLE):
@@ -169,13 +174,23 @@
         )
 
     def w_copy(turn, place):
-        if place < len(WAYS):
-            source, target = sendw.at[turn], recvw.at[turn, place]
-        else:
-            source, target = sendw.at[turn, 0], recvp.at[turn, place - len(WAYS)]
-        return remote(source, target, sendw_sem.at[turn, place], recvw_sem.at[turn, place], place)
-
-    def g_copy(way):
+        return remote(
+            sendw.at[turn], recvw.at[turn, place],
+            sendw_sem.at[place], recvw_sem.at[lax.rem(turn, 2), place], place,
+        )
+
+    def u_copy(turn, way):
+        return remote(
+            sendu.at[turn], recvu.at[turn, way],
+            sendu_sem.at[way], recvu_sem.at[lax.rem(turn, 2), way], way,
+        )
+
+    def g_copy(v, way):
+        return remote(
+            sendg.at[way, v], recvg.at[way, v], sendg_sem.at[way], recvg_sem.at[way], way
+        )
+
+    def g_whole(way):
         return remote(sendg.at[way], recvg.at[way], sendg_sem.at[way], recvg_sem.at[way], way)
 
     def t_copy(way):
@@ -193,6 +208,9 @@
 
     def begin_copy(copy):
         copy.start()
+
+    def settle(copy):
+        copy.wait_send()
 
     ways = range(len(WAYS))
     far = range(len(WAYS), len(CIRCLE))
@@ -211,36 +229,18 @@
             (8, LANES),
         )
 
-    def pack_w(turn, step):
+    def listed(step):
         tables = [hist[step, :, tile(j)] for j in range(tiles)]
         picked = [pick(tables, sidx[pair], 0) for pair in range(2)]
-        sendw[turn, 0] = jnp.concatenate([picked[0][0:4], picked[1][0:4]], axis=0)
-        for j in range(0, tiles, 2):
-            sendw[turn, 1 + j // 2] = jnp.concatenate([tables[j][0:4], tables[j + 1][0:4]], axis=0)
-
-    pack_w(0, 0)
-
-    loads[2].wait()
-    loads[3].wait()
-    agg = agg_ref[...]
-    member = (
-        jnp.broadcast_to(agg, (sizes_of, rows)) == lax.broadcasted_iota(jnp.int32, (sizes_of, rows), 0)
-    ).astype(jnp.float32)
-    counts = jnp.sum(member, axis=1, keepdims=True)
-    sizes = jnp.sum(member * counts, axis=0, keepdims=True)
-    tent = near_ref[...] * lax.rsqrt(sizes)
-    tent_ref[...] = tent
-    text[...] = jnp.zeros_like(text)
-    for c in range(3):
-        text[8 * c : 8 * c + modes, 0:rows] = tent_ref[modes * c : modes * (c + 1), :]
-    for pair in range(2):
-        for c in range(3):
-            sendt[pair, 8 * c : 8 * c + 8, :] = pick(
-                [text[8 * c : 8 * c + 8, tile(j)] for j in range(tiles)], sidx[pair], 0
-            )
+        return jnp.concatenate([picked[0][0:4], picked[1][0:4]], axis=0)
+
+    sendw[0] = listed(0)
 
     loads[4].wait()
     loads[5].wait()
+    inverse = invert_rows([diag_ref[p : p + 1, :] for p in range(9)])
+    for p in range(9):
+        dinv[p : p + 1, :] = inverse[p]
     rest_m[...] = jnp.zeros_like(rest_m)
     for u, places in enumerate(units):
         if len(places) * places[0][2] < 8:
@@ -250,28 +250,6 @@
             if count < 8:
                 rest_m[planes - 1, j, 0:count, :] = cols_ref[k : k + count, tile(j)].astype(jnp.float32)
 
-    inverse = invert_rows([diag_ref[p : p + 1, :] for p in range(9)])
-    for p in range(9):
-        dinv[p : p + 1, :] = inverse[p]
-    pl.semaphore_wait(barrier, greeters)
-    each_target(functools.partial(w_copy, 0), ORDER, begin_copy)
-    loads[6].wait()
-    for u, places in enumerate(units):
-        if len(places) * places[0][2] < 8:
-            mats[u] = jnp.zeros(mats.shape[1:], jnp.float32)
-        for at, k, count, j in places:
-            block = [off_v[p, k : k + count, tile(j)] for p in range(9)]
-            for r in range(3):
-                scale = [
-                    jnp.broadcast_to(dinv[3 * r + q : 3 * r + q + 1, tile(j)], (count, LANES))
-                    for q in range(3)
-                ]
-                for c in range(3):
-                    entry = scale[0] * block[c] + scale[1] * block[3 + c] + scale[2] * block[6 + c]
-                    mats[u, 3 * r + c, at : at + count, :] = entry
-                    if count < 8:
-                        rest_m[3 * r + c, j, 0:count, :] = entry
-
     def source(q, group, j):
         if 8 * (group + 1) > slots:
             return rest_m[q, j]
@@ -283,15 +261,55 @@
             return jnp.zeros((8, LANES), jnp.float32)
         return pick([source(q, group, j) for j in range(tiles)], sidx[pair], 0)
 
-    for pair in range(2):
-        for v in range(gunits):
+    for v, (cut, length) in enumerate(cuts):
+        loads[6 + v].wait()
+        for u, places in enumerate(units):
+            if not cut <= places[0][1] < cut + length:
+                continue
+            if len(places) * places[0][2] < 8:
+                mats[u] = jnp.zeros(mats.shape[1:], jnp.float32)
+            for at, k, count, j in places:
+                block = [off_v[p, k : k + count, tile(j)] for p in range(9)]
+                for r in range(3):
+                    scale = [
+                        jnp.broadcast_to(dinv[3 * r + q : 3 * r + q + 1, tile(j)], (count, LANES))
+                        for q in range(3)
+                    ]
+                    for c in range(3):
+                        entry = scale[0] * block[c] + scale[1] * block[3 + c] + scale[2] * block[6 + c]
+                        mats[u, 3 * r + c, at : at + count, :] = entry
+                        if count < 8:
+                            rest_m[3 * r + c, j, 0:count, :] = entry
+        for pair in (1, 0):
             for q in range(planes):
                 low = chosen(q, 2 * v, pair)
                 high = chosen(q, 2 * v + 1, pair)
                 sendg[2 * pair, v, q] = jnp.where(left, low, pltpu.roll(high, half, 1))
                 sendg[2 * pair + 1, v, q] = jnp.where(left, pltpu.roll(low, half, 1), high)
-        each_target(g_copy, (2 * pair, 2 * pair + 1), begin_copy)
-    each_target(t_copy, ways, begin_copy)
+            if v == 0 and pair == 1:
+                pl.semaphore_wait(barrier, greeters)
+                each_target(functools.partial(w_copy, 0), ORDER, begin_copy)
+            each_target(functools.partial(g_copy, v), (2 * pair, 2 * pair + 1), begin_copy)
+
+    def tentative():
+        loads[2].wait()
+        loads[3].wait()
+        agg = agg_ref[...]
+        member = (
+            jnp.broadcast_to(agg, (sizes_of, rows)) == lax.broadcasted_iota(jnp.int32, (sizes_of, rows), 0)
+        ).astype(jnp.float32)
+        counts = jnp.sum(member, axis=1, keepdims=True)
+        sizes = jnp.sum(member * counts, axis=0, keepdims=True)
+        tent_ref[...] = near_ref[...] * lax.rsqrt(sizes)
+        text[...] = jnp.zeros_like(text)
+        for c in range(3):
+            text[8 * c : 8 * c + modes, 0:rows] = tent_ref[modes * c : modes * (c + 1), :]
+        for pair in range(2):
+            for c in range(3):
+                sendt[pair, 8 * c : 8 * c + 8, :] = pick(
+                    [text[8 * c : 8 * c + 8, tile(j)] for j in range(tiles)], sidx[pair], 0
+                )
+        each_target(t_copy, ways, begin_copy)
 
     per = -(-len(units) // (BLOCKS - 1))
 
@@ -374,6 +392,9 @@
     def iterate(turn, unused):
         step = DEPTH * turn
         own_part(step)
+        sendu[turn] = listed(step + 1)
+        each_target(functools.partial(u_copy, turn), ways, begin_copy)
+        pl.when(turn == 0)(tentative)
 
         @pl.when(turn == 1)
         def _():
@@ -389,46 +410,38 @@
         lax.fori_loop(
             jnp.clip((turn - 1) * per, 0, len(units)), jnp.clip(turn * per, 0, len(units)), unit_products, 0
         )
+        each_target(functools.partial(w_copy, turn), ORDER, settle)
+        each_target(functools.partial(u_copy, turn), ways, settle)
         each_source(functools.partial(w_copy, turn), ways)
-        merged = [
-            halves(recvw[turn, 2 * pair, 0], recvw[turn, 2 * pair + 1, 0], pair) for pair in range(2)
-        ]
+        merged = [halves(recvw[turn, 2 * pair], recvw[turn, 2 * pair + 1], pair) for pair in range(2)]
         ghost_part(step, [[spread(merged[pair][c]) for pair in range(2)] for c in range(3)])
+        own_part(step + 1)
 
         @pl.when(turn == 0)
         def _():
-            each_source(g_copy, ways)
+            each_source(g_whole, ways)
             for way in ways:
                 for v in range(gunits):
                     gcol[way, v] = recvg[way, v, planes - 1].astype(jnp.int32)
 
-        inside = []
-        for way in ways:
-            tables = [
-                [
-                    spread(recvw[turn, way, 1 + i // 2, 4 * (i % 2) + c : 4 * (i % 2) + c + 1, :])
-                    for i in range(tiles)
-                ]
-                for c in range(3)
-            ]
-            inside.append(contribute_near(tables, 0, way))
-        own_part(step + 1)
-
         each_source(functools.partial(w_copy, turn), far)
 
         def packed(way, other):
             x, y = (WAYS[way][axis] + WAYS[other][axis] for axis in range(2))
-            return sendw[turn, 0] if (x, y) == (0, 0) else recvp[turn, FAR.index((x, y))]
+            return sendw[turn] if (x, y) == (0, 0) else recvw[turn, CIRCLE.index((x, y))]
 
         total = []
         for way in ways:
             rows_of = [
                 halves(packed(way, 2 * pair), packed(way, 2 * pair + 1), pair) for pair in range(2)
             ]
-            outside = contribute_near(
-                [[spread(rows_of[pair][c]) for pair in range(2)] for c in range(3)], tiles, way
+            total.append(
+                contribute_near(
+                    [[spread(rows_of[pair][c]) for pair in range(2)] for c in range(3)], tiles, way
+                )
             )
-            total.append([inside[way][r] + outside[r] for r in range(3)])
+        each_source(functools.partial(u_copy, turn), ways)
+        base = [halves(recvu[turn, 2 * pair], recvu[turn, 2 * pair + 1], pair) for pair in range(2)]
         later = [[], [], []]
         for r in range(3):
             for pair in range(2):
@@ -436,12 +449,12 @@
                 both = jnp.where(left, first, second) + pltpu.roll(
                     jnp.where(left, second, first), half, 1
                 )
-                later[r].append(spread(merged[pair][r] + jnp.sum(both, axis=0, keepdims=True)))
+                later[r].append(spread(base[pair][r] + jnp.sum(both, axis=0, keepdims=True)))
         ghost_part(step + 1, later)
 
         @pl.when(turn < BLOCKS - 1)
         def _():
-            pack_w(turn + 1, step + DEPTH)
+            sendw[turn + 1] = listed(step + DEPTH)
             each_target(functools.partial(w_copy, turn + 1), ORDER, begin_copy)
 
         return unused
@@ -461,55 +474,37 @@
     devices = n_slab * n_sub
     stat[0] = own
 
-    def stat_copy(step, source):
-        target = lax.rem(me + step, devices)
-        landing = lax.rem(me + devices - step, devices) if source else me
-        return pltpu.make_async_remote_copy(
-            src_ref=stat.at[0], dst_ref=stats.at[landing],
-            send_sem=ss_sem.at[step], recv_sem=rs_sem.at[landing],
+    def begin(step, unused):
+        target = lax.rem(me + jnp.where(2 * a < n_slab, devices - step, step), devices)
+        pltpu.make_async_remote_copy(
+            src_ref=stat.at[0], dst_ref=stats.at[me], send_sem=ss_sem, recv_sem=rs_sem,
             device_id={"slab": lax.div(target, n_sub), "sub": lax.rem(target, n_sub)},
             device_id_type=MESH,
-        )
-
-    def begin(step, unused):
-        stat_copy(step, False).start()
-        return unused
-
-    def arrive(step, unused):
-        stat_copy(step, True).wait_recv()
-        return unused
-
-    def sent(step, unused):
-        stat_copy(step, False).wait_send()
+        ).start()
         return unused
 
     lax.fori_loop(1, devices, begin, 0)
     stats[me] = own
-    lax.fori_loop(1, devices, arrive, 0)
+    others = stats.at[pl.ds(0, devices - 1)]
+    everything = pltpu.make_async_remote_copy(
+        src_ref=others, dst_ref=others, send_sem=ss_sem, recv_sem=rs_sem,
+        device_id={"slab": n_slab - 1 - a, "sub": n_sub - 1 - b}, device_id_type=MESH,
+    )
+    everything.wait_recv()
     whole = jnp.sum(stats[...], axis=0)
     latest = whole[:, 0:1]
     previous = whole[:, 1:2]
     rho_ref[...] = jnp.sqrt(latest / (previous + 1e-05))
 
-    lax.fori_loop(1, devices, sent, 0)
-    def settle(copy):
-        copy.wait_send()
-
-    each_target(g_copy, ways, settle)
+    everything.wait_send()
+    each_target(g_whole, ways, settle)
     each_target(t_copy, ways, settle)
-
-    def drain(turn, unused):
-        each_target(functools.partial(w_copy, turn), ORDER, settle)
-        return unused
-
-    lax.fori_loop(0, BLOCKS, drain, 0)
 
 
 def body(n_slab, n_sub, near_null, aggregates, diag_block, off_blocks, columns, sends, start_vector):
     slots, nine, rows = off_blocks.shape
     wide = rows + 2 * LANES
     count = len(unit_places(slots, rows // LANES))
-    parts = 1 + rows // (2 * LANES)
     gunits = -(-slots // 16)
     f32 = jnp.float32
     vmem = pl.BlockSpec(memory_space=pltpu.VMEM)
@@ -538,9 +533,10 @@
             pltpu.VMEM((24, wide), f32),
             pltpu.VMEM((ITERS + 1, 8, rows), f32),
             pltpu.VMEM((2, 8, LANES), jnp.int32),
-            pltpu.VMEM((BLOCKS, parts, 8, LANES), f32),
-            pltpu.VMEM((BLOCKS, len(WAYS), parts, 8, LANES), f32),
-            pltpu.VMEM((BLOCKS, len(FAR), 8, LANES), f32),
+            pltpu.VMEM((BLOCKS, 8, LANES), f32),
+            pltpu.VMEM((BLOCKS, len(CIRCLE), 8, LANES), f32),
+            pltpu.VMEM((BLOCKS, 8, LANES), f32),
+            pltpu.VMEM((BLOCKS, len(WAYS), 8, LANES), f32),
             pltpu.VMEM((len(WAYS), gunits, nine + 1, 8, LANES), f32),
             pltpu.VMEM((len(WAYS), gunits, nine + 1, 8, LANES), f32),
             pltpu.VMEM((len(WAYS), gunits, 8, LANES), jnp.int32),
@@ -548,15 +544,17 @@
             pltpu.VMEM((4, 24, LANES), f32),
             pltpu.VMEM((1, 1, LANES), f32),
             pltpu.VMEM((n_slab * n_sub, 1, LANES), f32),
-            dma((7,)),
-            dma((BLOCKS, len(CIRCLE))),
-            dma((BLOCKS, len(CIRCLE))),
-            dma((4,)),
-            dma((4,)),
-            dma((4,)),
-            dma((4,)),
-            dma((n_slab * n_sub,)),
-            dma((n_slab * n_sub,)),
+            dma((6 + gunits,)),
+            dma((len(CIRCLE),)),
+            dma((2, len(CIRCLE))),
+            dma((len(WAYS),)),
+            dma((2, len(WAYS))),
+            dma((len(WAYS),)),
+            dma((len(WAYS),)),
+            dma((len(WAYS),)),
+            dma((len(WAYS),)),
+            dma,
+            dma,
         ],
         compiler_params=pltpu.CompilerParams(collective_id=0, has_side_effects=True, vmem_limit_bytes=16777216),
         name="smooth",

time: 34.5 us -> 30.5 us (0.88)
  Pallas kernels: 33.7 us -> 29.6 us
    pallas_call x1, Pallas kernels: 32 us -> 28 us  [body(): pl.pallas_call(functools.partial(kernel, n_slab, n_sub), out_shape=(pltpu...]
where the time goes in v4:
time: 30.5 us; the launch traced here: 30.3 us
  Pallas kernels  29.6 us (97%)
  between operations  0.64 us (2%)
    pallas_call x1, Pallas kernels, body(): pl.pallas_call(functools.partial(kernel, n_slab, n_sub), out_shape=(pltpu...  28 us
    pallas_call x1, Pallas kernels, body(): pl.pallas_call(scale_kernel, out_shape=(jax.ShapeDtypeStruct((near_null.s...  1.63 us

profile of v4, /device:TPU:0, one launch (start us, length us, event | category | flops | bytes accessed | tf_op | source)
XLA Modules:
  0.0 30.3 jit_solution(2406996678679223592)
XLA Ops:
  0.6 28.0 %smooth.1 = (f32[18,13,8,128]{3,2,1,0:T(8,128)S(1)}, f32[18,512]{1,0:T(8,128)S(1)}, f32[1,1]{1,0:T(1,128)}) custom-call(f32[18,512]{1,0:T(8,128)} %near_hbm.1, s32[1,512]{1,0:T(1,128)} %bitcast.5, f32[9,512]{1,0:T(8,128)} %diag_hbm.1, f32[9,26,512]{2,1,0:T(8,128)} %bitcast.4, s32[26,512]{1,0:T(8,128)} %cols_hbm.1, s32[4,64]{1,0:T(4,128)} %sends_hbm.1, ...), custom_call_target="tpu_custom_call" | custom-call | tf_op jit(solution)/shard_map/smooth/pallas_call | solution.py:512
  28.6 1.6 %scale.1 = (bf16[18,26,512]{2,1,0:T(8,128)(2,1)}, bf16[18,512]{1,0:T(8,128)(2,1)}, f32[1,1]{1,0:T(1,128)}) custom-call(f32[18,13,8,128]{3,2,1,0:T(8,128)S(1)} %get-tuple-element.9.raw_ref, f32[18,512]{1,0:T(8,128)S(1)} %get-tuple-element.10.tent_ref, f32[1,1]{1,0:T(1,128)} %get-tuple-element.11.rho_ref), custom_call_target="tpu_custom_call" | custom-call | tf_op jit(solution)/shard_map/scale/pallas_call | solution.py:570

commit v5 on v1

v5 whole, which is shorter than its diff:
```python
import functools

import jax
import jax.numpy as jnp
from jax import lax
from jax.experimental import pallas as pl
from jax.experimental.pallas import tpu as pltpu
from jax.sharding import PartitionSpec as P

ITERS = 8
OMEGA = 4.0 / 3.0
LANES = 128
MESH = pl.DeviceIdType.MESH
LOAD_ORDER = [0, 1, 4, 5, 2, 3]
DEPTH = 2
BLOCKS = ITERS // DEPTH
WAYS = [(0, 1), (0, -1), (1, 0), (-1, 0)]
FAR = [(-1, -1), (-1, 1), (1, -1), (1, 1), (-2, 0), (2, 0), (0, -2), (0, 2)]
CIRCLE = WAYS + FAR
ORDER = list(range(len(WAYS), len(CIRCLE))) + list(range(len(WAYS)))


def lane_gather(table, lanes):
    return jnp.take_along_axis(table, lanes, axis=1, mode="promise_in_bounds")


def tile(number):
    return pl.ds(number * LANES, LANES)


def pick(tables, index, first):
    high = index >> 7
    low = index & (LANES - 1)
    out = jnp.zeros(index.shape, jnp.float32)
    for step, table in enumerate(tables):
        out = jnp.where(high == first + step, lane_gather(table, low), out)
    return out


def invert_rows(entries):
    cofactor = [
        entries[4] * entries[8] - entries[5] * entries[7],
        entries[5] * entries[6] - entries[3] * entries[8],
        entries[3] * entries[7] - entries[4] * entries[6],
        entries[2] * entries[7] - entries[1] * entries[8],
        entries[0] * entries[8] - entries[2] * entries[6],
        entries[1] * entries[6] - entries[0] * entries[7],
        entries[1] * entries[5] - entries[2] * entries[4],
        entries[2] * entries[3] - entries[0] * entries[5],
        entries[0] * entries[4] - entries[1] * entries[3],
    ]
    determinant = entries[0] * cofactor[0] + entries[1] * cofactor[1] + entries[2] * cofactor[2]
    return [
        cofactor[column * 3 + row] / determinant for row in range(3) for column in range(3)
    ]


def unit_places(slots, tiles):
    units = []
    for k in range(0, slots - 7, 8):
        for j in range(tiles):
            units.append([(0, k, 8, j)])
    rest = slots % 8
    if rest:
        share = 8 // rest
        for j in range(0, tiles, share):
            units.append(
                [
                    (rest * i, slots - rest, rest, j + i)
                    for i in range(min(share, tiles - j))
                ]
            )
    return units


def scale_kernel(raw_ref, tent_ref, rho_ref, off_ref, self_ref, out_rho_ref):
    slots, rows = off_ref.shape[1:]
    out_rho_ref[...] = rho_ref[...]
    inverse = OMEGA / rho_ref[...]
    factor = jnp.broadcast_to(-inverse, (8, LANES))
    places = unit_places(slots, rows // LANES)
    for j in range(rows // LANES):
        for entry in range(off_ref.shape[0]):
            parts = [
                (raw_ref[entry, u] * factor)[at : at + count]
                for u in range(len(places))
                for at, k, count, tile_number in places[u]
                if tile_number == j
            ]
            off_ref[entry, :, tile(j)] = jnp.concatenate(parts, axis=0).astype(off_ref.dtype)
    self_ref[...] = ((1.0 - inverse) * tent_ref[...]).astype(self_ref.dtype)


def kernel(
    n_slab, n_sub,
    near_hbm, agg_hbm, diag_hbm, off_hbm, cols_hbm, sends_hbm, start_hbm,
    raw_ref, tent_ref, rho_ref,
    near_ref, agg_ref, diag_ref, cols_ref, sends_ref, start_ref, off_v, cols_u, mats, rest_m, dinv, text, hist, sidx,
    sendw, recvw, sendu, recvu, mine, minecol, sendg, recvg, gcol, sendt, recvt, stat, stats,
    ss_sem, rs_sem,
):
    a = lax.axis_index("slab")
    b = lax.axis_index("sub")
    devices = n_slab * n_sub

    def power(
        off_sem, sendw_sem, recvw_sem, sendu_sem, recvu_sem, sendg_sem, recvg_sem, sendt_sem, recvt_sem
    ):
        slots, rows = cols_ref.shape
        half = sends_ref.shape[1]
        tiles = rows // LANES
        units = unit_places(slots, tiles)
        groups = -(-slots // 8)
        gunits, planes = sendg.shape[1:3]
        modes = near_ref.shape[0] // 3
        sizes_of = rows // 8
        barrier = pltpu.get_barrier_semaphore()
        def present(x, y):
            return (a + x >= 0) & (a + x < n_slab) & (b + y >= 0) & (b + y < n_sub)

        def greet(x, y):
            pl.semaphore_signal(
                barrier, inc=1, device_id={"slab": a + x, "sub": b + y}, device_id_type=MESH
            )

        def greet_any(step, unused):
            target = lax.rem(a * n_sub + b + step, n_slab * n_sub)
            greet(lax.div(target, n_sub) - a, lax.rem(target, n_sub) - b)
            return unused

        near = n_slab - 1 + n_sub - 1 <= ITERS + 2
        if near:
            for x, y in CIRCLE:
                pl.when(present(x, y))(functools.partial(greet, x, y))
            greeters = sum(present(x, y).astype(jnp.int32) for x, y in CIRCLE)
        else:
            lax.fori_loop(1, n_slab * n_sub, greet_any, 0)
            greeters = n_slab * n_sub - 1

        loads = [
            pltpu.make_async_copy(source, target, off_sem.at[number])
            for number, (source, target) in enumerate(
                (
                    (start_hbm, start_ref),
                    (sends_hbm, sends_ref),
                    (agg_hbm, agg_ref),
                    (near_hbm, near_ref),
                    (diag_hbm, diag_ref),
                    (cols_hbm, cols_ref),
                )
            )
        ]
        cuts = [(16 * v, min(16, slots - 16 * v)) for v in range(gunits)]
        loads += [
            pltpu.make_async_copy(
                off_hbm.at[:, pl.ds(k, count)], off_v.at[:, pl.ds(k, count)], off_sem.at[len(loads) + v]
            )
            for v, (k, count) in enumerate(cuts)
        ]
        for number in LOAD_ORDER + list(range(len(LOAD_ORDER), len(loads))):
            loads[number].start()

        def clear(place):
            cleared = [recvw.at[:, place]]
            if place < len(WAYS):
                cleared += [recvu.at[:, place], recvg.at[place], recvt.at[place]]
            for ref in cleared:
                ref[...] = jnp.zeros(ref.shape, jnp.float32)

        for place, (x, y) in enumerate(CIRCLE):
            pl.when(jnp.logical_not(present(-x, -y)))(functools.partial(clear, place))

        def remote(source, target, sent, came, place):
            x, y = CIRCLE[place]
            return pltpu.make_async_remote_copy(
                src_ref=source, dst_ref=target, send_sem=sent, recv_sem=came,
                device_id={"slab": a + x, "sub": b + y}, device_id_type=MESH,
            )

        def w_copy(turn, place):
            return remote(
                sendw.at[turn], recvw.at[turn, place],
                sendw_sem.at[place], recvw_sem.at[lax.rem(turn, 2), place], place,
            )

        def u_copy(turn, way):
            return remote(
                sendu.at[turn], recvu.at[turn, way],
                sendu_sem.at[way], recvu_sem.at[lax.rem(turn, 2), way], way,
            )

        def g_copy(v, way):
            return remote(
                sendg.at[way, v], recvg.at[way, v], sendg_sem.at[way], recvg_sem.at[way], way
            )

        def g_whole(way):
            return remote(sendg.at[way], recvg.at[way], sendg_sem.at[way], recvg_sem.at[way], way)

        def t_copy(way):
            return remote(sendt.at[way // 2], recvt.at[way], sendt_sem.at[way], recvt_sem.at[way], way)

        def each_target(make, places, act):
            for place in places:
                x, y = CIRCLE[place]
                pl.when(present(x, y))(functools.partial(lambda place: act(make(place)), place))

        def each_source(make, places):
            for place in places:
                x, y = CIRCLE[place]
                pl.when(present(-x, -y))(functools.partial(lambda place: make(place).wait_recv(), place))

        def begin_copy(copy):
            copy.start()

        def settle(copy):
            copy.wait_send()

        ways = range(len(WAYS))
        far = range(len(WAYS), len(CIRCLE))
        left = lax.broadcasted_iota(jnp.int32, (8, LANES), 1) < half

        hist[...] = jnp.zeros_like(hist)
        loads[0].wait()
        loads[1].wait()
        hist[0, 0:3, :] = start_ref[...]
        for pair in range(2):
            sidx[pair] = jnp.broadcast_to(
                jnp.concatenate(
                    [sends_ref[2 * pair : 2 * pair + 1, :], sends_ref[2 * pair + 1 : 2 * pair + 2, :]],
                    axis=1,
                ),
                (8, LANES),
            )

        def listed(step):
            tables = [hist[step, :, tile(j)] for j in range(tiles)]
            picked = [pick(tables, sidx[pair], 0) for pair in range(2)]
            return jnp.concatenate([picked[0][0:4], picked[1][0:4]], axis=0)

        sendw[...] = jnp.zeros_like(sendw)
        sendu[...] = jnp.zeros_like(sendu)
        sendw[0] = listed(0)

        loads[4].wait()
        loads[5].wait()
        inverse = invert_rows([diag_ref[p : p + 1, :] for p in range(9)])
        for p in range(9):
            dinv[p : p + 1, :] = inverse[p]
        rest_m[...] = jnp.zeros_like(rest_m)
        for u, places in enumerate(units):
            if len(places) * places[0][2] < 8:
                cols_u[u] = jnp.zeros((8, LANES), jnp.int32)
            for at, k, count, j in places:
                cols_u[u, at : at + count, :] = cols_ref[k : k + count, tile(j)]
                if count < 8:
                    rest_m[planes - 1, j, 0:count, :] = cols_ref[k : k + count, tile(j)].astype(jnp.float32)

        def source(q, group, j):
            if 8 * (group + 1) > slots:
                return rest_m[q, j]
            u = group * tiles + j
            return cols_u[u].astype(jnp.float32) if q == planes - 1 else mats[u, q]

        def chosen(q, group, pair):
            if group >= groups:
                return jnp.zeros((8, LANES), jnp.float32)
            return pick([source(q, group, j) for j in range(tiles)], sidx[pair], 0)

        for v, (cut, length) in enumerate(cuts):
            loads[6 + v].wait()
            for u, places in enumerate(units):
                if not cut <= places[0][1] < cut + length:
                    continue
                if len(places) * places[0][2] < 8:
                    mats[u] = jnp.zeros(mats.shape[1:], jnp.float32)
                for at, k, count, j in places:
                    block = [off_v[p, k : k + count, tile(j)] for p in range(9)]
                    for r in range(3):
                        scale = [
                            jnp.broadcast_to(dinv[3 * r + q : 3 * r + q + 1, tile(j)], (count, LANES))
                            for q in range(3)
                        ]
                        for c in range(3):
                            entry = scale[0] * block[c] + scale[1] * block[3 + c] + scale[2] * block[6 + c]
                            mats[u, 3 * r + c, at : at + count, :] = entry
                            if count < 8:
                                rest_m[3 * r + c, j, 0:count, :] = entry
            for pair in (1, 0):
                for q in range(planes):
                    low = chosen(q, 2 * v, pair)
                    high = chosen(q, 2 * v + 1, pair)
                    for group, listing in ((2 * v, low), (2 * v + 1, high)):
                        if group < groups and q < planes - 1:
                            mine[pair, group, q] = listing
                        elif group < groups:
                            minecol[pair, group] = listing.astype(jnp.int32)
                    sendg[2 * pair, v, q] = jnp.where(left, low, pltpu.roll(high, half, 1))
                    sendg[2 * pair + 1, v, q] = jnp.where(left, pltpu.roll(low, half, 1), high)
                if v == 0 and pair == 1:
                    pl.semaphore_wait(barrier, greeters)
                    each_target(functools.partial(w_copy, 0), ORDER, begin_copy)
                each_target(functools.partial(g_copy, v), (2 * pair, 2 * pair + 1), begin_copy)

        def tentative():
            loads[2].wait()
            loads[3].wait()
            agg = agg_ref[...]
            member = (
                jnp.broadcast_to(agg, (sizes_of, rows)) == lax.broadcasted_iota(jnp.int32, (sizes_of, rows), 0)
            ).astype(jnp.float32)
            counts = jnp.sum(member, axis=1, keepdims=True)
            sizes = jnp.sum(member * counts, axis=0, keepdims=True)
            tent_ref[...] = near_ref[...] * lax.rsqrt(sizes)
            text[...] = jnp.zeros_like(text)
            for c in range(3):
                text[8 * c : 8 * c + modes, 0:rows] = tent_ref[modes * c : modes * (c + 1), :]
            for pair in range(2):
                for c in range(3):
                    sendt[pair, 8 * c : 8 * c + 8, :] = pick(
                        [text[8 * c : 8 * c + 8, tile(j)] for j in range(tiles)], sidx[pair], 0
                    )
            each_target(t_copy, ways, begin_copy)

        per = -(-len(units) // (BLOCKS - 1))

        def spread(row):
            return jnp.broadcast_to(row, (8, LANES))

        def unit_products(u, unused):
            index = cols_u[u]
            for m in range(modes):
                picked = [
                    pick(
                        [
                            spread(text[8 * c + m : 8 * c + m + 1, tile(i)])
                            for i in range(tiles + 2)
                        ],
                        index,
                        0,
                    )
                    for c in range(3)
                ]
                for r in range(3):
                    raw_ref[modes * r + m, u] = (
                        mats[u, 3 * r] * picked[0]
                        + mats[u, 3 * r + 1] * picked[1]
                        + mats[u, 3 * r + 2] * picked[2]
                    )
            return unused

        def contribute(tables, first, u):
            index = cols_u[u]
            picked = [pick(tables[c], index, first) for c in range(3)]
            return [sum(mats[u, 3 * r + c] * picked[c] for c in range(3)) for r in range(3)]

        def contribute_near(tables, first, way):
            total = [None] * 3
            for v in range(gunits):
                index = gcol[way, v]
                picked = [pick(tables[c], index, first) for c in range(3)]
                for r in range(3):
                    term = sum(recvg[way, v, 3 * r + c] * picked[c] for c in range(3))
                    total[r] = term if total[r] is None else total[r] + term
            return total

        def contribute_mine(tables, first):
            total = [[None] * 3 for pair in range(2)]
            for pair in range(2):
                for group in range(groups):
                    index = minecol[pair, group]
                    picked = [pick(tables[c], index, first) for c in range(3)]
                    for r in range(3):
                        term = sum(mine[pair, group, 3 * r + c] * picked[c] for c in range(3))
                        total[pair][r] = term if group == 0 else total[pair][r] + term
            return total

        def own_tables(step):
            return [[spread(hist[step, c : c + 1, tile(i)]) for i in range(tiles)] for c in range(3)]

        def by_tile(terms):
            whole = [[None] * tiles for r in range(3)]
            for r in range(3):
                for u, places in enumerate(units):
                    if len(places) == 1 and places[0][2] == 8:
                        j = places[0][3]
                        old = whole[r][j]
                        whole[r][j] = terms[u][r] if old is None else old + terms[u][r]
                for j in range(tiles):
                    old = whole[r][j]
                    whole[r][j] = 0.0 if old is None else jnp.sum(old, axis=0, keepdims=True)
                for u, places in enumerate(units):
                    if not (len(places) == 1 and places[0][2] == 8):
                        for at, k, count, j in places:
                            whole[r][j] = whole[r][j] + jnp.sum(
                                terms[u][r][at : at + count], axis=0, keepdims=True
                            )
            return whole

        def own_part(step):
            tables = own_tables(step)
            inner = by_tile([contribute(tables, 0, u) for u in range(len(units))])
            for r in range(3):
                for j in range(tiles):
                    hist[step + 1, r : r + 1, tile(j)] = hist[step, r : r + 1, tile(j)] + inner[r][j]

        def ghost_part(step, tables):
            outer = by_tile([contribute(tables, tiles, u) for u in range(len(units))])
            for r in range(3):
                for j in range(tiles):
                    hist[step + 1, r : r + 1, tile(j)] = hist[step + 1, r : r + 1, tile(j)] + outer[r][j]

        def halves(first, second, pair):
            both = jnp.where(left, first, second)
            return [both[4 * pair + c : 4 * pair + c + 1] for c in range(3)]

        def iterate(turn, last):
            step = DEPTH * turn
            inner = contribute_mine(own_tables(step), 0)
            for pair in range(2):
                for r in range(3):
                    at = pl.ds(4 * pair + r, 1)
                    sendu[turn, at, :] = sendw[turn, at, :] + jnp.sum(inner[pair][r], axis=0, keepdims=True)
            each_target(functools.partial(u_copy, turn), ways, begin_copy)
            own_part(step)
            pl.when(turn == 0)(tentative)

            @pl.when(turn == 1)
            def _():
                each_source(t_copy, ways)
                for pair in range(2):
                    for c in range(3):
                        text[8 * c : 8 * c + 8, tile(tiles + pair)] = jnp.where(
                            left,
                            recvt[2 * pair, 8 * c : 8 * c + 8, :],
                            recvt[2 * pair + 1, 8 * c : 8 * c + 8, :],
                        )

            lax.fori_loop(
                jnp.clip((turn - 1) * per, 0, len(units)), jnp.clip(turn * per, 0, len(units)), unit_products, 0
            )
            each_target(functools.partial(w_copy, turn), ORDER, settle)
            each_target(functools.partial(u_copy, turn), ways, settle)
            each_source(functools.partial(w_copy, turn), ways)
            merged = [halves(recvw[turn, 2 * pair], recvw[turn, 2 * pair + 1], pair) for pair in range(2)]
            ghost_part(step, [[spread(merged[pair][c]) for pair in range(2)] for c in range(3)])
            if last:
                own_part(step + 1)
                stat[0, 1:2, :] = squares(step + 1)
            else:
                kept = listed(step + 1)
                inner = contribute_mine(own_tables(step + 1), 0)

            @pl.when(turn == 0)
            def _():
                each_source(g_whole, ways)
                for way in ways:
                    for v in range(gunits):
                        gcol[way, v] = recvg[way, v, planes - 1].astype(jnp.int32)

            each_source(functools.partial(w_copy, turn), far)

            def packed(way, other):
                x, y = (WAYS[way][axis] + WAYS[other][axis] for axis in range(2))
                return sendw[turn] if (x, y) == (0, 0) else recvw[turn, CIRCLE.index((x, y))]

            total = []
            for way in ways:
                rows_of = [
                    halves(packed(way, 2 * pair), packed(way, 2 * pair + 1), pair) for pair in range(2)
                ]
                total.append(
                    contribute_near(
                        [[spread(rows_of[pair][c]) for pair in range(2)] for c in range(3)], tiles, way
                    )
                )
            each_source(functools.partial(u_copy, turn), ways)
            base = [halves(recvu[turn, 2 * pair], recvu[turn, 2 * pair + 1], pair) for pair in range(2)]
            later = [[], [], []]
            for r in range(3):
                for pair in range(2):
                    first, second = total[2 * pair][r], total[2 * pair + 1][r]
                    both = jnp.where(left, first, second) + pltpu.roll(
                        jnp.where(left, second, first), half, 1
                    )
                    later[r].append(spread(base[pair][r] + jnp.sum(both, axis=0, keepdims=True)))
            if last:
                ghost_part(step + 1, later)
                return
            outer = contribute_mine(later, tiles)
            for pair in range(2):
                for r in range(3):
                    row = 4 * pair + r
                    sendw[turn + 1, row : row + 1, :] = kept[row : row + 1] + jnp.sum(
                        inner[pair][r] + outer[pair][r], axis=0, keepdims=True
                    )
            each_target(functools.partial(w_copy, turn + 1), ORDER, begin_copy)
            own_part(step + 1)
            ghost_part(step + 1, later)

        def squares(step):
            return jnp.sum(
                sum(hist[step, :, tile(j)] * hist[step, :, tile(j)] for j in range(tiles)),
                axis=0, keepdims=True,
            )

        def advance(turn, unused):
            iterate(turn, False)
            return unused

        lax.fori_loop(0, BLOCKS - 1, advance, 0)
        iterate(BLOCKS - 1, True)

        stat[0, 0:1, :] = squares(ITERS)
        me = a * n_sub + b

        def begin(step, unused):
            target = lax.rem(me + jnp.where(2 * a < n_slab, devices - step, step), devices)
            pltpu.make_async_remote_copy(
                src_ref=stat.at[0], dst_ref=stats.at[me], send_sem=ss_sem, recv_sem=rs_sem,
                device_id={"slab": lax.div(target, n_sub), "sub": lax.rem(target, n_sub)},
                device_id_type=MESH,
            ).start()
            return unused

        lax.fori_loop(1, devices, begin, 0, unroll=devices <= 64)
        stats[me] = stat[0]
        each_target(g_whole, ways, settle)
        each_target(t_copy, ways, settle)

    dma = pltpu.SemaphoreType.DMA
    ways = len(WAYS)
    pl.run_scoped(
        power,
        dma((6 + sendg.shape[1],)),
        dma((len(CIRCLE),)),
        dma((2, len(CIRCLE))),
        dma((ways,)),
        dma((2, ways)),
        dma((ways,)),
        dma((ways,)),
        dma((ways,)),
        dma((ways,)),
    )
    others = stats.at[pl.ds(0, devices - 1)]
    everything = pltpu.make_async_remote_copy(
        src_ref=others, dst_ref=others, send_sem=ss_sem, recv_sem=rs_sem,
        device_id={"slab": n_slab - 1 - a, "sub": n_sub - 1 - b}, device_id_type=MESH,
    )
    everything.wait_recv()
    whole = jnp.sum(stats[...], axis=0)
    total = jnp.sum(whole, axis=1, keepdims=True)
    latest = total[0:1]
    previous = total[1:2]
    rho_ref[...] = jnp.sqrt(latest / (previous + 1e-05))

    everything.wait_send()


def body(n_slab, n_sub, near_null, aggregates, diag_block, off_blocks, columns, sends, start_vector):
    slots, nine, rows = off_blocks.shape
    wide = rows + 2 * LANES
    count = len(unit_places(slots, rows // LANES))
    gunits = -(-slots // 16)
    f32 = jnp.float32
    vmem = pl.BlockSpec(memory_space=pltpu.VMEM)
    dma = pltpu.SemaphoreType.DMA
    raw, tentative, rho = pl.pallas_call(
        functools.partial(kernel, n_slab, n_sub),
        out_shape=(
            pltpu.VMEM((near_null.shape[0], count, 8, LANES), f32),
            pltpu.VMEM(near_null.shape, f32),
            jax.ShapeDtypeStruct((1, 1), f32),
        ),
        in_specs=[pl.BlockSpec(memory_space=pltpu.HBM)] * 7,
        out_specs=(vmem, vmem, vmem),
        scratch_shapes=[
            pltpu.VMEM(near_null.shape, f32),
            pltpu.VMEM((1, rows), jnp.int32),
            pltpu.VMEM(diag_block.shape, f32),
            pltpu.VMEM(columns.shape, jnp.int32),
            pltpu.VMEM(sends.shape, jnp.int32),
            pltpu.VMEM(start_vector.shape, f32),
            pltpu.VMEM((nine, slots, rows), f32),
            pltpu.VMEM((count, 8, LANES), jnp.int32),
            pltpu.VMEM((count, nine, 8, LANES), f32),
            pltpu.VMEM((nine + 1, rows // LANES, 8, LANES), f32),
            pltpu.VMEM((16, rows), f32),
            pltpu.VMEM((24, wide), f32),
            pltpu.VMEM((ITERS + 1, 8, rows), f32),
            pltpu.VMEM((2, 8, LANES), jnp.int32),
            pltpu.VMEM((BLOCKS, 8, LANES), f32),
            pltpu.VMEM((BLOCKS, len(CIRCLE), 8, LANES), f32),
            pltpu.VMEM((BLOCKS, 8, LANES), f32),
            pltpu.VMEM((BLOCKS, len(WAYS), 8, LANES), f32),
            pltpu.VMEM((2, -(-slots // 8), nine, 8, LANES), f32),
            pltpu.VMEM((2, -(-slots // 8), 8, LANES), jnp.int32),
            pltpu.VMEM((len(WAYS), gunits, nine + 1, 8, LANES), f32),
            pltpu.VMEM((len(WAYS), gunits, nine + 1, 8, LANES), f32),
            pltpu.VMEM((len(WAYS), gunits, 8, LANES), jnp.int32),
            pltpu.VMEM((2, 24, LANES), f32),
            pltpu.VMEM((4, 24, LANES), f32),
            pltpu.VMEM((1, 2, LANES), f32),
            pltpu.VMEM((n_slab * n_sub, 2, LANES), f32),
            dma,
            dma,
        ],
        compiler_params=pltpu.CompilerParams(collective_id=0, has_side_effects=True, vmem_limit_bytes=16777216),
        name="smooth",
    )(
        *[
            pltpu.with_memory_space_constraint(x, pltpu.HBM)
            for x in (
                near_null, aggregates.reshape(1, rows), diag_block, off_blocks.transpose(1, 0, 2),
                columns, sends, start_vector,
            )
        ]
    )
    prolong_off, prolong_self, rho = pl.pallas_call(
        scale_kernel,
        out_shape=(
            jax.ShapeDtypeStruct((near_null.shape[0], slots, rows), jnp.bfloat16),
            jax.ShapeDtypeStruct(near_null.shape, jnp.bfloat16),
            jax.ShapeDtypeStruct((1, 1), f32),
        ),
        in_specs=[vmem, vmem, vmem],
        out_specs=(vmem, vmem, vmem),
        compiler_params=pltpu.CompilerParams(vmem_limit_bytes=16777216),
        name="scale",
    )(raw, tentative, rho)
    return (prolong_off.transpose(1, 0, 2), prolong_self, rho.reshape(()))


def solution(mesh):
    placed = (
        P(None, ("slab", "sub")),
        P(("slab", "sub")),
        P(None, ("slab", "sub")),
        P(None, None, ("slab", "sub")),
        P(None, ("slab", "sub")),
        P(None, ("slab", "sub")),
        P(None, ("slab", "sub")),
    )
    return jax.shard_map(
        functools.partial(body, mesh.shape["slab"], mesh.shape["sub"]),
        mesh=mesh,
        in_specs=placed,
        out_specs=(P(None, None, ("slab", "sub")), P(None, ("slab", "sub")), P()),
        check_vma=False,
    )
```

time: 38.4 us -> 29 us (0.76)
  Pallas kernels: 37.6 us -> 28.2 us
    pallas_call x1, Pallas kernels: 35.9 us -> 26.5 us  [body(): pl.pallas_call(functools.partial(kernel, n_slab, n_sub), out_shape=(pltpu...]
where the time goes in v5:
time: 29 us; the launch traced here: 28.8 us
  Pallas kernels  28.2 us (97%)
  between operations  0.64 us (2%)
    pallas_call x1, Pallas kernels, body(): pl.pallas_call(functools.partial(kernel, n_slab, n_sub), out_shape=(pltpu...  26.5 us
    pallas_call x1, Pallas kernels, body(): pl.pallas_call(scale_kernel, out_shape=(jax.ShapeDtypeStruct((near_null.s...  1.63 us

profile of v5, /device:TPU:0, one launch (start us, length us, event | category | flops | bytes accessed | tf_op | source)
XLA Modules:
  0.0 28.8 jit_solution(15238502105951626978)
XLA Ops:
  0.6 26.5 %smooth.1 = (f32[18,13,8,128]{3,2,1,0:T(8,128)S(1)}, f32[18,512]{1,0:T(8,128)S(1)}, f32[1,1]{1,0:T(1,128)}) custom-call(f32[18,512]{1,0:T(8,128)} %near_hbm.1, s32[1,512]{1,0:T(1,128)} %bitcast.5, f32[9,512]{1,0:T(8,128)} %diag_hbm.1, f32[9,26,512]{2,1,0:T(8,128)} %bitcast.4, s32[26,512]{1,0:T(8,128)} %cols_hbm.1, s32[4,64]{1,0:T(4,128)} %sends_hbm.1, ...), custom_call_target="tpu_custom_call" | custom-call | tf_op jit(solution)/shard_map/smooth/pallas_call | solution.py:568
  27.2 1.6 %scale.1 = (bf16[18,26,512]{2,1,0:T(8,128)(2,1)}, bf16[18,512]{1,0:T(8,128)(2,1)}, f32[1,1]{1,0:T(1,128)}) custom-call(f32[18,13,8,128]{3,2,1,0:T(8,128)S(1)} %get-tuple-element.9.raw_ref, f32[18,512]{1,0:T(8,128)S(1)} %get-tuple-element.10.tent_ref, f32[1,1]{1,0:T(1,128)} %get-tuple-element.11.rho_ref), custom_call_target="tpu_custom_call" | custom-call | tf_op jit(solution)/shard_map/scale/pallas_call | solution.py:619

commit v6 on v5

--- a/solution.py
+++ b/solution.py
@@ -75,9 +75,9 @@
 
 def scale_kernel(raw_ref, tent_ref, rho_ref, off_ref, self_ref, out_rho_ref):
     slots, rows = off_ref.shape[1:]
-    out_rho_ref[...] = rho_ref[...]
+    out_rho_ref[...] = rho_ref[0:1, 0:1]
     inverse = OMEGA / rho_ref[...]
-    factor = jnp.broadcast_to(-inverse, (8, LANES))
+    factor = -inverse
     places = unit_places(slots, rows // LANES)
     for j in range(rows // LANES):
         for entry in range(off_ref.shape[0]):
@@ -88,7 +88,7 @@
                 if tile_number == j
             ]
             off_ref[entry, :, tile(j)] = jnp.concatenate(parts, axis=0).astype(off_ref.dtype)
-    self_ref[...] = ((1.0 - inverse) * tent_ref[...]).astype(self_ref.dtype)
+    self_ref[...] = ((1.0 - inverse[0:1, 0:1]) * tent_ref[...]).astype(self_ref.dtype)
 
 
 def kernel(
@@ -150,6 +150,7 @@
                 )
             )
         ]
+        deep = [min(8, -(-(slots - 16 * v) // 2)) for v in range(gunits)]
         cuts = [(16 * v, min(16, slots - 16 * v)) for v in range(gunits)]
         loads += [
             pltpu.make_async_copy(
@@ -159,6 +160,11 @@
         ]
         for number in LOAD_ORDER + list(range(len(LOAD_ORDER), len(loads))):
             loads[number].start()
+
+        for way in range(len(WAYS)):
+            for v in range(gunits):
+                if deep[v] < 8:
+                    recvg[way, v, :, deep[v] : 8, :] = jnp.zeros((planes, 8 - deep[v], LANES), jnp.float32)
 
         def clear(place):
             cleared = [recvw.at[:, place]]
@@ -190,12 +196,11 @@
             )
 
         def g_copy(v, way):
+            part = pl.ds(0, deep[v])
             return remote(
-                sendg.at[way, v], recvg.at[way, v], sendg_sem.at[way], recvg_sem.at[way], way
-            )
-
-        def g_whole(way):
-            return remote(sendg.at[way], recvg.at[way], sendg_sem.at[way], recvg_sem.at[way], way)
+                sendg.at[way, v, :, part], recvg.at[way, v, :, part],
+                sendg_sem.at[way, v], recvg_sem.at[way, v], way,
+            )
 
         def t_copy(way):
             return remote(sendt.at[way // 2], recvt.at[way], sendt_sem.at[way], recvt_sem.at[way], way)
@@ -286,21 +291,27 @@
                             mats[u, 3 * r + c, at : at + count, :] = entry
                             if count < 8:
                                 rest_m[3 * r + c, j, 0:count, :] = entry
-            for pair in (1, 0):
-                for q in range(planes):
-                    low = chosen(q, 2 * v, pair)
-                    high = chosen(q, 2 * v + 1, pair)
-                    for group, listing in ((2 * v, low), (2 * v + 1, high)):
-                        if group < groups and q < planes - 1:
-                            mine[pair, group, q] = listing
-                        elif group < groups:
-                            minecol[pair, group] = listing.astype(jnp.int32)
-                    sendg[2 * pair, v, q] = jnp.where(left, low, pltpu.roll(high, half, 1))
-                    sendg[2 * pair + 1, v, q] = jnp.where(left, pltpu.roll(low, half, 1), high)
-                if v == 0 and pair == 1:
-                    pl.semaphore_wait(barrier, greeters)
-                    each_target(functools.partial(w_copy, 0), ORDER, begin_copy)
-                each_target(functools.partial(g_copy, v), (2 * pair, 2 * pair + 1), begin_copy)
+        def pack_rows(v, pair):
+            count = deep[v]
+            for q in range(planes):
+                low = chosen(q, 2 * v, pair)
+                high = chosen(q, 2 * v + 1, pair)
+                for group, listing in ((2 * v, low), (2 * v + 1, high)):
+                    if group < groups and q < planes - 1:
+                        mine[pair, group, q] = listing
+                    elif group < groups:
+                        minecol[pair, group] = listing.astype(jnp.int32)
+                if count < 8:
+                    high = jnp.concatenate([low[count:8], high[0:count]], axis=0)
+                sendg[2 * pair, v, q] = jnp.where(left, low, pltpu.roll(high, half, 1))
+                sendg[2 * pair + 1, v, q] = jnp.where(left, pltpu.roll(low, half, 1), high)
+
+        for number, (v, pair) in enumerate([(v, pair) for v in range(gunits) for pair in (0, 1)]):
+            pack_rows(v, pair)
+            if number == 0:
+                pl.semaphore_wait(barrier, greeters)
+                each_target(functools.partial(w_copy, 0), ORDER, begin_copy)
+            each_target(functools.partial(g_copy, v), (2 * pair, 2 * pair + 1), begin_copy)
 
         def tentative():
             loads[2].wait()
@@ -453,7 +464,8 @@
 
             @pl.when(turn == 0)
             def _():
-                each_source(g_whole, ways)
+                for v in range(gunits):
+                    each_source(functools.partial(g_copy, v), ways)
                 for way in ways:
                     for v in range(gunits):
                         gcol[way, v] = recvg[way, v, planes - 1].astype(jnp.int32)
@@ -525,7 +537,8 @@
 
         lax.fori_loop(1, devices, begin, 0, unroll=devices <= 64)
         stats[me] = stat[0]
-        each_target(g_whole, ways, settle)
+        for v in range(gunits):
+            each_target(functools.partial(g_copy, v), ways, settle)
         each_target(t_copy, ways, settle)
 
     dma = pltpu.SemaphoreType.DMA
@@ -537,8 +550,8 @@
         dma((2, len(CIRCLE))),
         dma((ways,)),
         dma((2, ways)),
-        dma((ways,)),
-        dma((ways,)),
+        dma((ways, sendg.shape[1])),
+        dma((ways, sendg.shape[1])),
         dma((ways,)),
         dma((ways,)),
     )
@@ -552,7 +565,7 @@
     total = jnp.sum(whole, axis=1, keepdims=True)
     latest = total[0:1]
     previous = total[1:2]
-    rho_ref[...] = jnp.sqrt(latest / (previous + 1e-05))
+    rho_ref[...] = jnp.broadcast_to(jnp.sqrt(latest / (previous + 1e-05)), rho_ref.shape)
 
     everything.wait_send()
 
@@ -570,7 +583,7 @@
         out_shape=(
             pltpu.VMEM((near_null.shape[0], count, 8, LANES), f32),
             pltpu.VMEM(near_null.shape, f32),
-            jax.ShapeDtypeStruct((1, 1), f32),
+            pltpu.VMEM((8, LANES), f32),
         ),
         in_specs=[pl.BlockSpec(memory_space=pltpu.HBM)] * 7,
         out_specs=(vmem, vmem, vmem),

time: 29 us -> 27.4 us (0.945)
  Pallas kernels: 28.2 us -> 26.5 us
    pallas_call x1, Pallas kernels: 26.5 us -> 25.6 us  [body(): pl.pallas_call(functools.partial(kernel, n_slab, n_sub), out_shape=(pltpu...]
    pallas_call x1, Pallas kernels: 1.63 us -> 0.93 us  [body(): pl.pallas_call(scale_kernel, out_shape=(jax.ShapeDtypeStruct((near_null.s...]
where the time goes in v6:
time: 27.4 us; the launch traced here: 27.2 us
  Pallas kernels  26.5 us (97%)
  between operations  0.64 us (2%)
    pallas_call x1, Pallas kernels, body(): pl.pallas_call(functools.partial(kernel, n_slab, n_sub), out_shape=(pltpu...  25.6 us
    pallas_call x1, Pallas kernels, body(): pl.pallas_call(scale_kernel, out_shape=(jax.ShapeDtypeStruct((near_null.s...  0.93 us

profile of v6, /device:TPU:0, one launch (start us, length us, event | category | flops | bytes accessed | tf_op | source)
XLA Modules:
  0.0 27.2 jit_solution(4626658486231853317)
XLA Ops:
  0.6 25.6 %smooth.1 = (f32[18,13,8,128]{3,2,1,0:T(8,128)S(1)}, f32[18,512]{1,0:T(8,128)S(1)}, f32[8,128]{1,0:T(8,128)S(1)}) custom-call(f32[18,512]{1,0:T(8,128)} %near_hbm.1, s32[1,512]{1,0:T(1,128)} %bitcast.5, f32[9,512]{1,0:T(8,128)} %diag_hbm.1, f32[9,26,512]{2,1,0:T(8,128)} %bitcast.4, s32[26,512]{1,0:T(8,128)} %cols_hbm.1, s32[4,64]{1,0:T(4,128)} %sends_hbm.1, ...), custom_call_target="tpu_custom_call" | custom-call | tf_op jit(solution)/shard_map/smooth/pallas_call | solution.py:581
  26.2 0.9 %scale.1 = (bf16[18,26,512]{2,1,0:T(8,128)(2,1)}, bf16[18,512]{1,0:T(8,128)(2,1)}, f32[1,1]{1,0:T(1,128)}) custom-call(f32[18,13,8,128]{3,2,1,0:T(8,128)S(1)} %get-tuple-element.9.raw_ref, f32[18,512]{1,0:T(8,128)S(1)} %get-tuple-element.10.tent_ref, f32[8,128]{1,0:T(8,128)S(1)} %get-tuple-element.11.rho_ref), custom_call_target="tpu_custom_call" | custom-call | tf_op jit(solution)/shard_map/scale/pallas_call | solution.py:632

commit v7 on v6

--- a/solution.py
+++ b/solution.py
@@ -130,7 +130,8 @@
 
         near = n_slab - 1 + n_sub - 1 <= ITERS + 2
         if near:
-            for x, y in CIRCLE:
+            for place in ORDER:
+                x, y = CIRCLE[place]
                 pl.when(present(x, y))(functools.partial(greet, x, y))
             greeters = sum(present(x, y).astype(jnp.int32) for x, y in CIRCLE)
         else:
@@ -184,14 +185,17 @@
             )
 
         def w_copy(turn, place):
+            x, y = CIRCLE[place]
+            part = pl.ds(4, 4) if y == 0 else pl.ds(0, 4) if x == 0 else pl.ds(0, 8)
             return remote(
-                sendw.at[turn], recvw.at[turn, place],
+                sendw.at[turn, part], recvw.at[turn, place, part],
                 sendw_sem.at[place], recvw_sem.at[lax.rem(turn, 2), place], place,
             )
 
         def u_copy(turn, way):
+            part = pl.ds(4 * (way // 2), 4)
             return remote(
-                sendu.at[turn], recvu.at[turn, way],
+                sendu.at[turn, part], recvu.at[turn, way, part],
                 sendu_sem.at[way], recvu_sem.at[lax.rem(turn, 2), way], way,
             )
 
@@ -422,8 +426,9 @@
                     hist[step + 1, r : r + 1, tile(j)] = hist[step + 1, r : r + 1, tile(j)] + outer[r][j]
 
         def halves(first, second, pair):
-            both = jnp.where(left, first, second)
-            return [both[4 * pair + c : 4 * pair + c + 1] for c in range(3)]
+            part = pl.ds(4 * pair, 4)
+            both = jnp.where(left[0:4], first[part, :], second[part, :])
+            return [both[c : c + 1] for c in range(3)]
 
         def iterate(turn, last):
             step = DEPTH * turn
@@ -453,11 +458,11 @@
             each_target(functools.partial(w_copy, turn), ORDER, settle)
             each_target(functools.partial(u_copy, turn), ways, settle)
             each_source(functools.partial(w_copy, turn), ways)
-            merged = [halves(recvw[turn, 2 * pair], recvw[turn, 2 * pair + 1], pair) for pair in range(2)]
+            merged = [halves(recvw.at[turn, 2 * pair], recvw.at[turn, 2 * pair + 1], pair) for pair in range(2)]
             ghost_part(step, [[spread(merged[pair][c]) for pair in range(2)] for c in range(3)])
             if last:
                 own_part(step + 1)
-                stat[0, 1:2, :] = squares(step + 1)
+                stat[1] = squares(step + 1)
             else:
                 kept = listed(step + 1)
                 inner = contribute_mine(own_tables(step + 1), 0)
@@ -474,7 +479,7 @@
 
             def packed(way, other):
                 x, y = (WAYS[way][axis] + WAYS[other][axis] for axis in range(2))
-                return sendw[turn] if (x, y) == (0, 0) else recvw[turn, CIRCLE.index((x, y))]
+                return sendw.at[turn] if (x, y) == (0, 0) else recvw.at[turn, CIRCLE.index((x, y))]
 
             total = []
             for way in ways:
@@ -487,7 +492,7 @@
                     )
                 )
             each_source(functools.partial(u_copy, turn), ways)
-            base = [halves(recvu[turn, 2 * pair], recvu[turn, 2 * pair + 1], pair) for pair in range(2)]
+            base = [halves(recvu.at[turn, 2 * pair], recvu.at[turn, 2 * pair + 1], pair) for pair in range(2)]
             later = [[], [], []]
             for r in range(3):
                 for pair in range(2):
@@ -523,7 +528,10 @@
         lax.fori_loop(0, BLOCKS - 1, advance, 0)
         iterate(BLOCKS - 1, True)
 
-        stat[0, 0:1, :] = squares(ITERS)
+        latest, previous = squares(ITERS), stat[1]
+        stat[0] = jnp.where(left[0:1], latest, previous) + pltpu.roll(
+            jnp.where(left[0:1], previous, latest), half, 1
+        )
         me = a * n_sub + b
 
         def begin(step, unused):
@@ -562,9 +570,9 @@
     )
     everything.wait_recv()
     whole = jnp.sum(stats[...], axis=0)
-    total = jnp.sum(whole, axis=1, keepdims=True)
-    latest = total[0:1]
-    previous = total[1:2]
+    first = lax.broadcasted_iota(jnp.int32, (1, LANES), 1) < sends_ref.shape[1]
+    latest = jnp.sum(jnp.where(first, whole, 0.0), axis=1, keepdims=True)
+    previous = jnp.sum(jnp.where(first, 0.0, whole), axis=1, keepdims=True)
     rho_ref[...] = jnp.broadcast_to(jnp.sqrt(latest / (previous + 1e-05)), rho_ref.shape)
 
     everything.wait_send()
@@ -613,8 +621,8 @@
             pltpu.VMEM((len(WAYS), gunits, 8, LANES), jnp.int32),
             pltpu.VMEM((2, 24, LANES), f32),
             pltpu.VMEM((4, 24, LANES), f32),
-            pltpu.VMEM((1, 2, LANES), f32),
-            pltpu.VMEM((n_slab * n_sub, 2, LANES), f32),
+            pltpu.VMEM((2, 1, LANES), f32),
+            pltpu.VMEM((n_slab * n_sub, 1, LANES), f32),
             dma,
             dma,
         ],

time: 27.4 us -> 27.3 us (level)
  no operation moved by 1% of the time
where the time goes in v7:
time: 27.3 us; the launch traced here: 27.1 us
  Pallas kernels  26.5 us (97%)
  between operations  0.64 us (2%)
    pallas_call x1, Pallas kernels, body(): pl.pallas_call(functools.partial(kernel, n_slab, n_sub), out_shape=(pltpu...  25.5 us
    pallas_call x1, Pallas kernels, body(): pl.pallas_call(scale_kernel, out_shape=(jax.ShapeDtypeStruct((near_null.s...  0.93 us

profile of v7, /device:TPU:0, one launch (start us, length us, event | category | flops | bytes accessed | tf_op | source)
XLA Modules:
  0.0 27.1 jit_solution(11034032580045580678)
XLA Ops:
  0.6 25.5 %smooth.1 = (f32[18,13,8,128]{3,2,1,0:T(8,128)S(1)}, f32[18,512]{1,0:T(8,128)S(1)}, f32[8,128]{1,0:T(8,128)S(1)}) custom-call(f32[18,512]{1,0:T(8,128)} %near_hbm.1, s32[1,512]{1,0:T(1,128)} %bitcast.5, f32[9,512]{1,0:T(8,128)} %diag_hbm.1, f32[9,26,512]{2,1,0:T(8,128)} %bitcast.4, s32[26,512]{1,0:T(8,128)} %cols_hbm.1, s32[4,64]{1,0:T(4,128)} %sends_hbm.1, ...), custom_call_target="tpu_custom_call" | custom-call | tf_op jit(solution)/shard_map/smooth/pallas_call | solution.py:589
  26.2 0.9 %scale.1 = (bf16[18,26,512]{2,1,0:T(8,128)(2,1)}, bf16[18,512]{1,0:T(8,128)(2,1)}, f32[1,1]{1,0:T(1,128)}) custom-call(f32[18,13,8,128]{3,2,1,0:T(8,128)S(1)} %get-tuple-element.9.raw_ref, f32[18,512]{1,0:T(8,128)S(1)} %get-tuple-element.10.tent_ref, f32[8,128]{1,0:T(8,128)S(1)} %get-tuple-element.11.rho_ref), custom_call_target="tpu_custom_call" | custom-call | tf_op jit(solution)/shard_map/scale/pallas_call | solution.py:640
